TPU v7x, 32 devices: a whole 2x2x4 slice. The times are simulated.
32 devices in a mesh: dp: 8 (over z, x), expert: 4 (over y, core).
Axes of the slice: x: 2, y: 2, z: 4, core: 2. Of those that a mesh axis runs over, the one named last changes fastest.
Arguments:
- tokens: bfloat16 [4096, 2048], P(('dp', 'expert')), may hold values from -6 to 6
- out_grad: bfloat16 [4096, 2048], P(('dp', 'expert')), may hold values from -3 to 3
- z_weight: float32 [4096], P(('dp', 'expert')), may hold values from 0.1 to 1
- router_weight: bfloat16 [2048, 128], replicated, may hold values from -0.125 to 0.125
- expert_ids: int32 [4096, 4], P(('dp', 'expert')), may hold values from 0 to 127, as said below
- gate_up_weight: bfloat16 [4, 2048, 3072], P('expert'), may hold values from -0.125 to 0.125
- down_weight: bfloat16 [4, 1536, 2048], P('expert'), may hold values from -0.15625 to 0.15625
Outputs:
- token_grad: bfloat16 [4096, 2048], P(('dp', 'expert'))
- router_grad: float32 [2048, 128], replicated
- gate_up_grad: bfloat16 [4, 2048, 3072], P('expert', 'dp')
- down_grad: bfloat16 [4, 1536, 2048], P('expert', 'dp')
Inputs may be any that keep to these rules, and one draw needn't show every extreme that they name: `expert_ids`: each row names 4 different experts. Experts 0 to 3 are the ones in flight. The 128 rows of one device name any one expert in flight at most 64 times; in every data group some expert in flight is named exactly 64 times by the rows of each device of the group.
All inputs are finite; a program needn't handle non-finite values.
Results may differ from a plain program's by a relative error of at most 0.019.
Values may be sent and summed in bfloat16 or wider, within the bound.
A program may use at most 192 MiB of HBM per device.

v0:
```python
import jax
import jax.numpy as jnp
from jax import lax
from jax.sharding import PartitionSpec as P


def expert_rows(rows_in, rows_grad, w_gateup, w_down, acc_gateup, acc_down):
    hidden_units = w_down.shape[0]
    pre_act = jnp.dot(rows_in, w_gateup, preferred_element_type=jnp.float32)
    gate_pre = pre_act[:, :hidden_units]
    up_pre = pre_act[:, hidden_units:]
    activated = jax.nn.silu(gate_pre)
    hidden = (activated * up_pre).astype(jnp.bfloat16)
    expert_out = jnp.dot(hidden, w_down, preferred_element_type=jnp.float32).astype(jnp.bfloat16)
    hidden_grad = lax.dot_general(
        rows_grad, w_down, (((1,), (1,)), ((), ())), preferred_element_type=jnp.float32
    )
    acc_down = lax.dot_general(
        hidden, rows_grad, (((0,), (0,)), ((), ())), preferred_element_type=jnp.float32
    )
    sigmoid_gate = jax.nn.sigmoid(gate_pre)
    gate_grad = hidden_grad * up_pre * sigmoid_gate * (1.0 + gate_pre * (1.0 - sigmoid_gate))
    up_grad = hidden_grad * activated
    pre_grad = jnp.concatenate([gate_grad, up_grad], axis=1).astype(jnp.bfloat16)
    acc_gateup = lax.dot_general(
        rows_in, pre_grad, (((0,), (0,)), ((), ())), preferred_element_type=jnp.float32
    )
    input_grad = lax.dot_general(
        pre_grad, w_gateup, (((1,), (1,)), ((), ())), preferred_element_type=jnp.float32
    ).astype(jnp.bfloat16)
    return (acc_gateup, acc_down, expert_out, input_grad)


def split_pair(values):
    upper = values.astype(jnp.bfloat16)
    lower = (values - upper.astype(jnp.float32)).astype(jnp.bfloat16)
    return jnp.stack([upper, lower], axis=-1)


def join_pair(pair):
    return pair[..., 0].astype(jnp.float32) + pair[..., 1].astype(jnp.float32)


def per_device(tokens, out_grad, z_weight, router_weight, expert_ids, gate_up_weight, down_weight):
    tok_count, width = tokens.shape
    top_count = expert_ids.shape[1]
    routed = router_weight.shape[1]
    flight = lax.axis_size("expert")
    capacity = tok_count // 2
    w_gateup = gate_up_weight[0]
    w_down = down_weight[0]
    hidden_units = w_down.shape[0]
    logits = jnp.dot(tokens, router_weight, preferred_element_type=jnp.float32)
    choose = expert_ids[:, :, None] == jnp.arange(routed, dtype=jnp.int32)[None, None, :]
    selected = jnp.sum(jnp.where(choose, logits[:, None, :], 0.0), axis=2)
    sel_exp = jnp.exp(selected)
    probs = sel_exp / jnp.sum(sel_exp, axis=1, keepdims=True)
    log_total = jnp.log(jnp.sum(jnp.exp(logits), axis=1))
    flat_ids = expert_ids.reshape(-1)
    slot_count = tok_count * top_count
    member = (flat_ids[:, None] == jnp.arange(flight, dtype=jnp.int32)[None, :]).astype(jnp.int32)
    ranks = jnp.sum((jnp.cumsum(member, axis=0) - 1) * member, axis=1)
    in_flight = flat_ids < flight
    position = jnp.where(in_flight, flat_ids * capacity + ranks, flight * capacity)
    source_slot = (
        jnp.zeros((flight * capacity,), jnp.int32)
        .at[position]
        .set(jnp.arange(slot_count, dtype=jnp.int32), mode="drop")
    )
    filled = jnp.zeros((flight * capacity,), jnp.bool_).at[position].set(True, mode="drop")
    source_tok = source_slot // top_count
    send_in = jnp.where(filled[:, None], tokens[source_tok], 0)
    slot_prob = jnp.where(filled, probs.reshape(-1)[source_slot], 0.0)
    counts = jnp.sum(member, axis=0)
    count_msg = jnp.stack([counts // 128, counts % 128], axis=1).astype(jnp.bfloat16)
    send_raw = jnp.where(filled[:, None], out_grad[source_tok], 0)
    prob_pair = split_pair(slot_prob)
    recv_in, recv_raw, recv_prob, recv_counts = (
        lax.all_to_all(
            send_in.reshape(flight, capacity, width),
            "expert",
            split_axis=0,
            concat_axis=0,
            tiled=True,
        ),
        lax.all_to_all(
            send_raw.reshape(flight, capacity, width),
            "expert",
            split_axis=0,
            concat_axis=0,
            tiled=True,
        ),
        lax.all_to_all(
            prob_pair.reshape(flight, capacity, 2),
            "expert",
            split_axis=0,
            concat_axis=0,
            tiled=True,
        ),
        lax.all_to_all(count_msg, "expert", split_axis=0, concat_axis=0, tiled=True),
    )
    sources = recv_in.shape[0]
    total_rows = sources * capacity
    flat_in = recv_in.reshape(total_rows, width)
    flat_raw = recv_raw.reshape(total_rows, width)
    row_prob = join_pair(recv_prob.reshape(total_rows, 2))
    flat_grad = (row_prob[:, None] * flat_raw.astype(jnp.float32)).astype(jnp.bfloat16)
    acc_gateup, acc_down, produced, back_rows = expert_rows(
        flat_in,
        flat_grad,
        w_gateup,
        w_down,
        jnp.zeros((width, 2 * hidden_units), jnp.float32),
        jnp.zeros((hidden_units, width), jnp.float32),
    )
    slot_at = jnp.where(in_flight, position, 0)
    row_score = jnp.sum(flat_raw.astype(jnp.float32) * produced.astype(jnp.float32), axis=1)
    score_pair = split_pair(row_score)
    home_dx, home_pair = (
        lax.all_to_all(
            back_rows.reshape(sources, capacity, width),
            "expert",
            split_axis=0,
            concat_axis=0,
            tiled=True,
        ),
        lax.all_to_all(
            score_pair.reshape(sources, capacity, 2),
            "expert",
            split_axis=0,
            concat_axis=0,
            tiled=True,
        ),
    )
    flat_dx = home_dx.reshape(flight * capacity, width)
    flat_score = join_pair(home_pair.reshape(flight * capacity, 2))
    scores = jnp.where(in_flight, flat_score[slot_at], 0.0).reshape(tok_count, top_count)
    slot_dx = jnp.where(in_flight[:, None], flat_dx[slot_at], 0).reshape(
        tok_count, top_count, width
    )
    mean_score = jnp.sum(probs * scores, axis=1, keepdims=True)
    sel_grad = probs * (scores - mean_score)
    z_grad = 2.0 * z_weight[:, None] * log_total[:, None] * jnp.exp(logits - log_total[:, None])
    logit_grad = (z_grad + jnp.sum(jnp.where(choose, sel_grad[:, :, None], 0.0), axis=1)).astype(
        jnp.bfloat16
    )
    token_grad = (
        jnp.sum(slot_dx.astype(jnp.float32), axis=1)
        + lax.dot_general(
            logit_grad, router_weight, (((1,), (1,)), ((), ())), preferred_element_type=jnp.float32
        )
    ).astype(jnp.bfloat16)
    router_part = lax.dot_general(
        tokens, logit_grad, (((0,), (0,)), ((), ())), preferred_element_type=jnp.float32
    )
    router_grad = lax.psum(router_part, ("dp", "expert"))
    part_gateup = acc_gateup.astype(jnp.bfloat16)
    part_down = acc_down.astype(jnp.bfloat16)
    gate_up_grad, down_grad = (
        lax.psum_scatter(part_gateup[None], "dp", scatter_dimension=1, tiled=True).astype(
            jnp.float32
        ),
        lax.psum_scatter(part_down[None], "dp", scatter_dimension=1, tiled=True).astype(
            jnp.float32
        ),
    )
    return (
        token_grad,
        router_grad,
        gate_up_grad.astype(jnp.bfloat16),
        down_grad.astype(jnp.bfloat16),
    )


def solution(mesh):
    return jax.shard_map(
        per_device,
        mesh=mesh,
        in_specs=(
            P(("dp", "expert"), None),
            P(("dp", "expert"), None),
            P(("dp", "expert")),
            P(),
            P(("dp", "expert"), None),
            P("expert", None, None),
            P("expert", None, None),
        ),
        out_specs=(
            P(("dp", "expert"), None),
            P(),
            P("expert", "dp", None),
            P("expert", "dp", None),
        ),
        check_vma=False,
    )
```

profile of v0, /device:TPU:0, one launch (start us, length us, event | category | flops | bytes accessed | tf_op | source)
XLA Modules:
  0.0 440.1 jit_solution(1820209398362379599)
XLA Ops:
  13.3 2.4 scatter_custom_fusion.1
  15.8 2.4 scatter_custom_fusion
  23.2 4.4 all-to-all-start.2
  29.0 13.1 %all-to-all-done.2 = bf16[4,64,2048]{2,1,0:T(8,128)(2,1)S(1)} async-done(((bf16[4,64,2048]{2,1,0:T(8,128)(2,1)}), bf16[4,64,2048]{2,1,0:T(8,128)(2,1)S(1)}, u32[]{:S(2)}, u32[]{:S(2)}) %all-to-all-start.2) | async-done | bytes 1048608 | tf_op jit(solution)/shard_map/all_to_all | solution.py:79
  42.0 3.5 all-to-all-start.1
  45.6 9.7 %fusion.2 = f32[256,3072]{1,0:T(8,128)} fusion(bf16[256,2048]{1,0:T(8,128)(2,1)S(1)} %bitcast.81, bf16[1,2048,3072]{2,1,0:T(8,128)(2,1)} %param.12), kind=kOutput, calls=%fused_computation.9 | convolution fusion | flops 3221225472 | bytes 16777216 | tf_op jit(solution)/shard_map/dot_general | solution.py:9
  55.2 2.3 multiply_convert_fusion.1
  57.6 2.4 all-to-all-done.1
  60.0 4.8 %fusion.24 = f32[256]{0:T(256)S(1)} fusion(bf16[256,1536]{1,0:T(8,128)(2,1)S(1)} %multiply_convert_fusion.1, bf16[1,1536,2048]{2,1,0:T(8,128)(2,1)} %param.13, bf16[256,2048]{1,0:T(8,128)(2,1)S(1)} %bitcast.80), kind=kOutput, calls=%fused_computation.35 | convolution fusion | flops 1613233920 | bytes 8127488 | tf_op jit(solution)/shard_map/dot_general | solution.py:14
  65.4 3.4 all-to-all-start.4
  69.4 3.0 all-to-all-done.4
  72.4 3.5 gather_fusion.4
  82.8 3.2 all-to-all-start
  91.2 4.4 %fusion.4 = bf16[1,1536,2048]{2,1,0:T(8,128)(2,1)} fusion(bf16[256,1536]{1,0:T(8,128)(2,1)S(1)} %multiply_convert_fusion.1, bf16[256,2048]{1,0:T(8,128)(2,1)S(1)} %fusion.22), kind=kOutput, calls=%fused_computation.13 | convolution fusion | flops 1613758464 | bytes 8126464 | tf_op jit(solution)/shard_map/dot_general | solution.py:18
  96.1 6.0 %multiply_convert_fusion.3 = (bf16[256,1536]{1,0:T(8,128)(2,1)S(1)}, bf16[256,1536]{1,0:T(8,128)(2,1)S(1)}) fusion(f32[256,3072]{1,0:T(8,128)} %fusion.2, bf16[256,2048]{1,0:T(8,128)(2,1)S(1)} %bitcast.85, bf16[1,1536,2048]{2,1,0:T(8,128)(2,1)} %param.13), kind=kOutput, calls=%fused_computation.32 | convolution fusion | flops 1615724544 | bytes 12058624 | tf_op jit(solution)/shard_map/dot_general | solution.py:15
  102.1 6.6 %convert_bitcast_fusion = bf16[1,2048,3072]{2,1,0:T(8,128)(2,1)} fusion(bf16[256,2048]{1,0:T(8,128)(2,1)S(1)} %bitcast.82, bf16[256,1536]{1,0:T(8,128)(2,1)S(1)} %get-tuple-element.31, bf16[256,1536]{1,0:T(8,128)(2,1)S(1)} %get-tuple-element.30), kind=kOutput, calls=%fused_computation.11 | convolution fusion | flops 3230662656 | bytes 15204352 | tf_op jit(solution)/shard_map/dot_general | solution.py:25
  108.7 9.0 %fusion.18 = bf16[256,2048]{1,0:T(8,128)(2,1)} fusion(bf16[1,2048,3072]{2,1,0:T(8,128)(2,1)} %param.12, bf16[256,1536]{1,0:T(8,128)(2,1)S(1)} %get-tuple-element.31, bf16[256,1536]{1,0:T(8,128)(2,1)S(1)} %get-tuple-element.30), kind=kOutput, calls=%fused_computation.22 | convolution fusion | flops 3224895488 | bytes 15204352 | tf_op jit(solution)/shard_map/dot_general | solution.py:28
  117.8 3.9 all-to-all-start.3
  121.7 229.6 %all-reduce.2.cloned.1.call-done = f32[2048,128]{0,1:T(8,128)} async-done(((f32[2048,128]{0,1:T(8,128)}), f32[2048,128]{0,1:T(8,128)}) %all-reduce.2.cloned.1.call-update) | async-done | bytes 1048592 | tf_op jit(solution)/shard_map/psum | solution.py:156
  351.2 2.6 copy.55
  353.8 2.5 gather_fusion.3
  356.3 2.2 gather.29
  358.6 5.6 %convert_reduce_fusion = f32[128,2048]{1,0:T(8,128)S(1)} fusion(bf16[128,4,2048]{2,1,0:T(4,128)(2,1)} %gather.29, pred[128,4]{1,0:T(8,128)(4,1)S(1)} %copy-done.6), kind=kLoop, calls=%fused_computation.18 | loop fusion | flops 2883584 | bytes 3146240 | tf_op jit(solution)/shard_map/reduce_sum | solution.py:148
  365.3 67.3 %reduce-scatter.3.cloned.1.call-done = bf16[1,256,3072]{2,1,0:T(8,128)(2,1)} async-done(((bf16[1,2048,3072]{2,1,0:T(8,128)(2,1)}), bf16[1,256,3072]{2,1,0:T(8,128)(2,1)}) %reduce-scatter.3.cloned.1.call-update) | async-done | bytes 1572880 | tf_op jit(solution)/shard_map/reduce_scatter | solution.py:160
  (97 shorter events, 26.4 us)
Async XLA Ops:
  8.0 10.9 %copy-start = (bf16[128,2048]{1,0:T(8,128)(2,1)S(1)}, bf16[128,2048]{1,0:T(8,128)(2,1)}, u32[]{:S(2)}) copy-start(bf16[128,2048]{1,0:T(8,128)(2,1)} %param.7) | copy-start | bytes 1572868
  10.6 0.6 copy-start.5
  18.2 0.7 copy-start.11
  18.9 1.4 copy-start.2
  23.2 4.4 %copy-start.3 = (bf16[2048,128]{1,0:T(8,128)(2,1)S(1)}, bf16[2048,128]{1,0:T(8,128)(2,1)}, u32[]{:S(2)}) copy-start(bf16[2048,128]{1,0:T(8,128)(2,1)} %param.10) | copy-start | bytes 1572868
  23.2 4.9 %copy-start.7 = (s32[128,4]{0,1:T(4,128)S(1)}, s32[128,4]{0,1:T(4,128)}, u32[]{:S(2)}) copy-start(s32[128,4]{0,1:T(4,128)} %param.11) | copy-start | bytes 6148
  23.2 5.1 %copy-start.12 = (f32[128]{0:T(128)S(1)}, f32[128]{0:T(128)}, u32[]{:S(2)}) copy-start(f32[128]{0:T(128)} %param.9) | copy-start | bytes 1540
  23.2 18.8 %all-to-all-start.2 = ((bf16[4,64,2048]{2,1,0:T(8,128)(2,1)}), bf16[4,64,2048]{2,1,0:T(8,128)(2,1)S(1)}, u32[]{:S(2)}, u32[]{:S(2)}) async-start(bf16[4,64,2048]{2,1,0:T(8,128)(2,1)} %get-tuple-element.38), calls=%async_computation.2 | async-start | bytes 2097152 | tf_op jit(solution)/shard_map/all_to_all | solution.py:79
  28.1 44.3 %copy-start.9 = (s32[1024]{0:T(1024)}, s32[1024]{0:T(1024)S(1)}, u32[]{:S(2)}) copy-start(s32[1024]{0:T(1024)S(1)} %pad_clamp_fusion) | copy-start | bytes 12292
  42.0 17.9 %all-to-all-start.1 = ((bf16[4,64,2048]{2,1,0:T(8,128)(2,1)}), bf16[4,64,2048]{2,1,0:T(8,128)(2,1)S(1)}, u32[]{:S(2)}, u32[]{:S(2)}) async-start(bf16[4,64,2048]{2,1,0:T(8,128)(2,1)} %get-tuple-element.39), calls=%async_computation.1 | async-start | bytes 2097152 | tf_op jit(solution)/shard_map/all_to_all | solution.py:86
  65.4 6.9 %all-to-all-start.4 = ((bf16[4,64,2]{1,2,0:T(2,128)(2,1)}), bf16[4,64,2]{1,2,0:T(2,128)(2,1)S(1)}, u32[]{:S(2)}, u32[]{:S(2)}) async-start(bf16[4,64,2]{1,2,0:T(2,128)(2,1)} %copy.51), calls=%async_computation.4 | async-start | bytes 4096 | tf_op jit(solution)/shard_map/all_to_all | solution.py:127
  77.3 0.6 copy-start.8
  82.8 6.9 %all-to-all-start = ((bf16[4,64,2]{1,2,0:T(2,128)(2,1)}), bf16[4,64,2]{1,2,0:T(2,128)(2,1)S(1)}, u32[]{:S(2)}, u32[]{:S(2)}) async-start(bf16[4,64,2]{1,2,0:T(2,128)(2,1)} %copy.49), calls=%async_computation | async-start | bytes 4096 | tf_op jit(solution)/shard_map/all_to_all | solution.py:93
  86.0 265.2 %all-reduce.2.cloned.1.call-start = ((), (), s32[]{:S(2)}) async-start(), calls=%async_computation.7 | async-start | bytes 2097152 | tf_op jit(solution)/shard_map/psum | solution.py:156
  89.2 276.1 %reduce-scatter.5.cloned.1.call-start = ((), (), s32[]{:S(2)}) async-start(), calls=%async_computation.9 | async-start | bytes 7077888 | tf_op jit(solution)/shard_map/reduce_scatter | solution.py:163
  95.7 336.9 %reduce-scatter.3.cloned.1.call-start = ((), (), s32[]{:S(2)}) async-start(), calls=%async_computation.8 | async-start | bytes 14155776 | tf_op jit(solution)/shard_map/reduce_scatter | solution.py:160
  117.8 236.0 %copy-start.10 = (s32[1024]{0:T(1024)S(1)}, s32[1024]{0:T(1024)}, u32[]{:S(2)}) copy-start(s32[1024]{0:T(1024)} %copy-done.9) | copy-start | bytes 12292
  117.8 236.0 %all-to-all-start.3 = ((bf16[4,64,2048]{2,1,0:T(8,128)(2,1)}), bf16[4,64,2048]{2,1,0:T(8,128)(2,1)S(1)}, u32[]{:S(2)}, u32[]{:S(2)}) async-start(bf16[4,64,2048]{2,1,0:T(8,128)(2,1)} %bitcast.9), calls=%async_computation.3 | async-start | bytes 2097152 | tf_op jit(solution)/shard_map/all_to_all | solution.py:120
  356.3 2.3 copy-start.6
  356.3 76.3 %copy-start.1 = (bf16[128,2048]{1,0:T(8,128)(2,1)S(1)}, bf16[128,2048]{1,0:T(8,128)(2,1)}, u32[]{:S(2)}) copy-start(bf16[128,2048]{1,0:T(8,128)(2,1)} %param.7) | copy-start | bytes 1572868
  358.6 5.6 %copy-start.4 = (bf16[2048,128]{1,0:T(8,128)(2,1)S(1)}, bf16[2048,128]{1,0:T(8,128)(2,1)}, u32[]{:S(2)}) copy-start(bf16[2048,128]{1,0:T(8,128)(2,1)} %param.10) | copy-start | bytes 1572868
Sparse Core Ops, SparseCore 0:
  92.6 258.5 all-reduce.1
Sparse Core Ops, SparseCore 1:
  95.8 123.6 reduce-scatter.4
  223.5 209.1 reduce-scatter.2
where the time goes:
time: 441 us; the launch traced here: 440 us
  waiting for transfers between devices  316 us (72%)
  matrix products  43.3 us (10%)
  local copies, waits for them, and re-layouts  26.9 us (6%)
  other arithmetic  19.7 us (4%)
  starting transfers between devices  18.5 us (4%)
  between operations  15.8 us (4%)
    psum x1, waiting for transfers between devices, per_device(): router_grad = lax.psum(router_part, ('dp', 'expert'))  230 us
    reduce_scatter x1, waiting for transfers between devices, per_device(): lax.psum_scatter(part_gateup[None], 'dp', scatter_dimension=1, tiled=True)  67.3 us
    all_to_all x1, waiting for transfers between devices, per_device(): lax.all_to_all(send_in.reshape(flight, capacity, width), 'expert', split_...  13.1 us
    dot_general x1, matrix products, expert_rows(): pre_act = jnp.dot(rows_in, w_gateup, preferred_element_type=jnp.float32)  9.69 us
    dot_general x1, matrix products, expert_rows(): lax.dot_general(pre_grad, w_gateup, (((1,), (1,)), ((), ())), preferred_e...  9.05 us
  transfers between devices with their start and end apart: 8, of which 6 were waited for; matrix products, arithmetic and copies ran while one was open for 13% of the time, Pallas kernels for 0%

commit v1 on v0

--- a/solution.py
+++ b/solution.py
@@ -1,34 +1,274 @@
+import functools
+
 import jax
 import jax.numpy as jnp
 from jax import lax
+from jax.experimental import pallas as pl
+from jax.experimental.pallas import tpu as pltpu
 from jax.sharding import PartitionSpec as P
 
-
-def expert_rows(rows_in, rows_grad, w_gateup, w_down, acc_gateup, acc_down):
+F32 = jnp.float32
+BF16 = jnp.bfloat16
+MESH = pl.DeviceIdType.MESH
+
+
+def ring_order(count):
+    inner = max(k for k in range(1, count + 1) if count % k == 0 and k * k <= count)
+    outer = count // inner
+    if inner == 1 or outer % 2:
+        return list(range(count))
+    order = []
+    for row in range(outer):
+        cols = list(range(1, inner))
+        order += [row * inner + col for col in (cols if row % 2 == 0 else cols[::-1])]
+    return order + [row * inner for row in range(outer)][::-1]
+
+
+def lookup(table, key):
+    value = jnp.int32(0)
+    for slot, entry in enumerate(table):
+        value = value + jnp.where(key == slot, jnp.int32(entry), jnp.int32(0))
+    return value
+
+
+def grads_kernel(
+    copies, flight, order,
+    xt_ref, pg_ref, ht_ref, dy_ref, rp_ref,
+    gu_ref, dn_ref, rout_ref,
+    gu_buf, dn_buf, rx_e, rsum, rx_d, rfull,
+    send_sem, recv_sem, es_send, es_recv, ds_send, ds_recv, dg_send, dg_recv, eg_send, eg_recv,
+):
+    d = lax.axis_index("dp")
+    e = lax.axis_index("expert")
+    n = copies
+    place = [order.index(i) for i in range(n)]
+    pos = lookup(place, d)
+    right = lookup(order, lax.rem(pos + 1, n))
+    left = lookup(order, lax.rem(pos + n - 1, n))
+    towards = (right, left)
+
+    barrier = pltpu.get_barrier_semaphore()
+    for k in range(1, n):
+        pl.semaphore_signal(barrier, inc=1, device_id=(lax.rem(d + k, n), e), device_id_type=MESH)
+    for k in range(1, flight):
+        pl.semaphore_signal(barrier, inc=1, device_id=(d, lax.rem(e + k, flight)), device_id_type=MESH)
+    pl.semaphore_wait(barrier, n + flight - 2)
+
+    gu_rows = gu_ref.shape[1]
+    half_rows = gu_rows // 2
+    dn_rows = dn_ref.shape[1]
+    gu_cols = gu_ref.shape[2] // 2
+    dn_cols = dn_ref.shape[2] // 2
+    piece_e = rsum.shape[0]
+    piece_d = rx_d.shape[1]
+
+    def owner_at(way, step):
+        if way == 0:
+            return lookup(order, lax.rem(pos + 2 * n - 1 - step, n))
+        return lookup(order, lax.rem(pos + 1 + step, n))
+
+    def own(way, part, owner):
+        if part < 2:
+            start = pl.multiple_of(owner * gu_rows + part * half_rows, half_rows)
+            return jnp.dot(
+                xt_ref[pl.ds(start, half_rows), :],
+                pg_ref[:, way * gu_cols:(way + 1) * gu_cols],
+                preferred_element_type=F32,
+            )
+        start = pl.multiple_of(owner * dn_rows, dn_rows)
+        return jnp.dot(
+            ht_ref[pl.ds(start, dn_rows), :],
+            dy_ref[:, way * dn_cols:(way + 1) * dn_cols],
+            preferred_element_type=F32,
+        )
+
+    def slot(way, part, step):
+        return gu_buf.at[way, part, step] if part < 2 else dn_buf.at[way, step]
+
+    def hop(way, part, step):
+        return pltpu.make_async_remote_copy(
+            src_ref=slot(way, part, step),
+            dst_ref=slot(way, part, step + 1),
+            send_sem=send_sem.at[way, part, step],
+            recv_sem=recv_sem.at[way, part, step],
+            device_id=(towards[way], e),
+            device_id_type=MESH,
+        )
+
+    def share_e(k):
+        to = lax.rem(e + k, flight)
+        return pltpu.make_async_remote_copy(
+            src_ref=rp_ref.at[pl.ds(pl.multiple_of(to * piece_e, piece_e), piece_e), :],
+            dst_ref=rx_e.at[k - 1],
+            send_sem=es_send.at[k - 1], recv_sem=es_recv.at[k - 1],
+            device_id=(d, to), device_id_type=MESH,
+        )
+
+    def share_d(k):
+        to = lax.rem(d + k, n)
+        return pltpu.make_async_remote_copy(
+            src_ref=rsum.at[pl.ds(pl.multiple_of(to * piece_d, piece_d), piece_d), :],
+            dst_ref=rx_d.at[k - 1],
+            send_sem=ds_send.at[k - 1], recv_sem=ds_recv.at[k - 1],
+            device_id=(to, e), device_id_type=MESH,
+        )
+
+    def gather_d(k, source):
+        rows = pl.ds(pl.multiple_of(e * piece_e + source * piece_d, piece_d), piece_d)
+        return pltpu.make_async_remote_copy(
+            src_ref=rfull.at[rows, :], dst_ref=rfull.at[rows, :],
+            send_sem=dg_send.at[k - 1], recv_sem=dg_recv.at[k - 1],
+            device_id=(lax.rem(d + k, n), e), device_id_type=MESH,
+        )
+
+    def gather_e(k, source):
+        rows = pl.ds(pl.multiple_of(source * piece_e, piece_e), piece_e)
+        return pltpu.make_async_remote_copy(
+            src_ref=rfull.at[rows, :], dst_ref=rfull.at[rows, :],
+            send_sem=eg_send.at[k - 1], recv_sem=eg_recv.at[k - 1],
+            device_id=(d, lax.rem(e + k, flight)), device_id_type=MESH,
+        )
+
+    for part in range(3):
+        for way in range(2):
+            slot(way, part, 0)[...] = own(way, part, owner_at(way, 0)).astype(BF16)
+            hop(way, part, 0).start()
+    for k in range(1, flight):
+        share_e(k).start()
+
+    def middle(step, carry):
+        for part in range(3):
+            for way in range(2):
+                hop(way, part, step - 1).wait_recv()
+                here = slot(way, part, step)
+                here[...] = (
+                    here[...].astype(F32) + own(way, part, owner_at(way, step))
+                ).astype(BF16)
+                hop(way, part, step).start()
+
+        @pl.when(step == 1)
+        def _():
+            total = rp_ref[pl.ds(pl.multiple_of(e * piece_e, piece_e), piece_e), :]
+            for k in range(1, flight):
+                share_e(k).wait_recv()
+                total = total + rx_e[k - 1]
+            rsum[...] = total
+            for k in range(1, n):
+                share_d(k).start()
+
+        @pl.when(step == 2)
+        def _():
+            total = rsum[pl.ds(pl.multiple_of(d * piece_d, piece_d), piece_d), :]
+            for k in range(1, n):
+                share_d(k).wait_recv()
+                total = total + rx_d[k - 1]
+            rfull[pl.ds(pl.multiple_of(e * piece_e + d * piece_d, piece_d), piece_d), :] = total
+            for k in range(1, n):
+                gather_d(k, d).start()
+
+        @pl.when(step == 3)
+        def _():
+            for k in range(1, n):
+                gather_d(k, lax.rem(d + n - k, n)).wait_recv()
+            for k in range(1, flight):
+                gather_e(k, e).start()
+
+        return carry
+
+    lax.fori_loop(1, n - 1, middle, 0)
+
+    for k in range(1, flight):
+        gather_e(k, lax.rem(e + flight - k, flight)).wait_recv()
+    rout_ref[...] = rfull[...]
+    for part in range(3):
+        for way in range(2):
+            hop(way, part, n - 2).wait_recv()
+            total = slot(way, part, n - 1)[...].astype(F32) + own(way, part, d)
+            if part < 2:
+                gu_ref[
+                    0, part * half_rows:(part + 1) * half_rows, way * gu_cols:(way + 1) * gu_cols
+                ] = total.astype(BF16)
+            else:
+                dn_ref[0, :, way * dn_cols:(way + 1) * dn_cols] = total.astype(BF16)
+
+    def drain(step, carry):
+        for part in range(3):
+            for way in range(2):
+                hop(way, part, step).wait_send()
+        return carry
+
+    lax.fori_loop(0, n - 1, drain, 0)
+    for k in range(1, n):
+        share_d(k).wait_send()
+        gather_d(k, d).wait_send()
+    for k in range(1, flight):
+        share_e(k).wait_send()
+        gather_e(k, e).wait_send()
+
+
+def reduce_grads(copies, flight, xt, pre_grad, ht, dyk, router_part):
+    width, rows = xt.shape
+    gate_up = pre_grad.shape[1]
+    hidden = ht.shape[0]
+    routed = router_part.shape[1]
+    n = copies
+    gu_rows, dn_rows = width // n, hidden // n
+    piece_e = width // flight
+    piece_d = piece_e // n
+    dma = pltpu.SemaphoreType.DMA
+    vmem = pl.BlockSpec(memory_space=pltpu.VMEM)
+    return pl.pallas_call(
+        functools.partial(grads_kernel, n, flight, ring_order(n)),
+        out_shape=(
+            jax.ShapeDtypeStruct((1, gu_rows, gate_up), BF16),
+            jax.ShapeDtypeStruct((1, dn_rows, width), BF16),
+            jax.ShapeDtypeStruct((width, routed), F32),
+        ),
+        in_specs=[vmem] * 5,
+        out_specs=(vmem,) * 3,
+        scratch_shapes=[
+            pltpu.VMEM((2, 2, n, gu_rows // 2, gate_up // 2), BF16),
+            pltpu.VMEM((2, n, dn_rows, width // 2), BF16),
+            pltpu.VMEM((flight - 1, piece_e, routed), F32),
+            pltpu.VMEM((piece_e, routed), F32),
+            pltpu.VMEM((n - 1, piece_d, routed), F32),
+            pltpu.VMEM((width, routed), F32),
+            dma((2, 3, n - 1)), dma((2, 3, n - 1)),
+            dma((flight - 1,)), dma((flight - 1,)),
+            dma((n - 1,)), dma((n - 1,)),
+            dma((n - 1,)), dma((n - 1,)),
+            dma((flight - 1,)), dma((flight - 1,)),
+        ],
+        compiler_params=pltpu.CompilerParams(
+            collective_id=0, has_side_effects=True, vmem_limit_bytes=50 * 2**20
+        ),
+        cost_estimate=pl.CostEstimate(
+            flops=2 * rows * width * (gate_up + hidden),
+            bytes_accessed=2 * (width * gate_up + hidden * width) // n,
+            transcendentals=0,
+        ),
+        name="grads",
+    )(xt, pre_grad, ht, dyk, router_part)
+
+def expert_rows(rows_in, rows_grad, w_gateup, w_down):
     hidden_units = w_down.shape[0]
-    pre_act = jnp.dot(rows_in, w_gateup, preferred_element_type=jnp.float32)
+    pre_act = jnp.dot(rows_in, w_gateup, preferred_element_type=F32)
     gate_pre = pre_act[:, :hidden_units]
     up_pre = pre_act[:, hidden_units:]
     activated = jax.nn.silu(gate_pre)
-    hidden = (activated * up_pre).astype(jnp.bfloat16)
-    expert_out = jnp.dot(hidden, w_down, preferred_element_type=jnp.float32).astype(jnp.bfloat16)
+    hidden = (activated * up_pre).astype(BF16)
+    expert_out = jnp.dot(hidden, w_down, preferred_element_type=F32).astype(BF16)
     hidden_grad = lax.dot_general(
-        rows_grad, w_down, (((1,), (1,)), ((), ())), preferred_element_type=jnp.float32
-    )
-    acc_down = lax.dot_general(
-        hidden, rows_grad, (((0,), (0,)), ((), ())), preferred_element_type=jnp.float32
+        rows_grad, w_down, (((1,), (1,)), ((), ())), preferred_element_type=F32
     )
     sigmoid_gate = jax.nn.sigmoid(gate_pre)
     gate_grad = hidden_grad * up_pre * sigmoid_gate * (1.0 + gate_pre * (1.0 - sigmoid_gate))
     up_grad = hidden_grad * activated
-    pre_grad = jnp.concatenate([gate_grad, up_grad], axis=1).astype(jnp.bfloat16)
-    acc_gateup = lax.dot_general(
-        rows_in, pre_grad, (((0,), (0,)), ((), ())), preferred_element_type=jnp.float32
-    )
+    pre_grad = jnp.concatenate([gate_grad, up_grad], axis=1).astype(BF16)
     input_grad = lax.dot_general(
-        pre_grad, w_gateup, (((1,), (1,)), ((), ())), preferred_element_type=jnp.float32
-    ).astype(jnp.bfloat16)
-    return (acc_gateup, acc_down, expert_out, input_grad)
+        pre_grad, w_gateup, (((1,), (1,)), ((), ())), preferred_element_type=F32
+    ).astype(BF16)
+    return (hidden, pre_grad, expert_out, input_grad)
 
 
 def split_pair(values):
@@ -105,14 +345,7 @@
     flat_raw = recv_raw.reshape(total_rows, width)
     row_prob = join_pair(recv_prob.reshape(total_rows, 2))
     flat_grad = (row_prob[:, None] * flat_raw.astype(jnp.float32)).astype(jnp.bfloat16)
-    acc_gateup, acc_down, produced, back_rows = expert_rows(
-        flat_in,
-        flat_grad,
-        w_gateup,
-        w_down,
-        jnp.zeros((width, 2 * hidden_units), jnp.float32),
-        jnp.zeros((hidden_units, width), jnp.float32),
-    )
+    hidden, pre_grad, produced, back_rows = expert_rows(flat_in, flat_grad, w_gateup, w_down)
     slot_at = jnp.where(in_flight, position, 0)
     row_score = jnp.sum(flat_raw.astype(jnp.float32) * produced.astype(jnp.float32), axis=1)
     score_pair = split_pair(row_score)
@@ -153,23 +386,10 @@
     router_part = lax.dot_general(
         tokens, logit_grad, (((0,), (0,)), ((), ())), preferred_element_type=jnp.float32
     )
-    router_grad = lax.psum(router_part, ("dp", "expert"))
-    part_gateup = acc_gateup.astype(jnp.bfloat16)
-    part_down = acc_down.astype(jnp.bfloat16)
-    gate_up_grad, down_grad = (
-        lax.psum_scatter(part_gateup[None], "dp", scatter_dimension=1, tiled=True).astype(
-            jnp.float32
-        ),
-        lax.psum_scatter(part_down[None], "dp", scatter_dimension=1, tiled=True).astype(
-            jnp.float32
-        ),
-    )
-    return (
-        token_grad,
-        router_grad,
-        gate_up_grad.astype(jnp.bfloat16),
-        down_grad.astype(jnp.bfloat16),
-    )
+    gate_up_grad, down_grad, router_grad = reduce_grads(
+        lax.axis_size("dp"), flight, flat_in.T, pre_grad, hidden.T, flat_grad, router_part
+    )
+    return (token_grad, router_grad, gate_up_grad, down_grad)
 
 
 def solution(mesh):

time: 441 us -> 325 us (0.74)
  waiting for transfers between devices: 316 us -> 18.6 us
  Pallas kernels: 0 us -> 197 us
  between operations: 15.8 us -> 0.99 us
  local copies, waits for them, and re-layouts: 26.9 us -> 35.5 us
  matrix products: 43.3 us -> 34.8 us
    psum x1 -> x0, waiting for transfers between devices: 230 us -> none  [per_device(): router_grad = lax.psum(router_part, ('dp', 'expert'))]
    pallas_call x0 -> x1, Pallas kernels: none -> 197 us  [reduce_grads(): pl.pallas_call(functools.partial(grads_kernel, n, flight, ring_order(n)),...]
    reduce_scatter x2 -> x0, waiting for transfers between devices: 67.3 us -> none  [the longest x1 67.3 us: per_device(): lax.psum_scatter(part_gateup[None], 'dp', scatter_dimension=1, tiled=True)]
    dot_general x4 -> x2, matrix products: 25.5 us -> 16.9 us  [the longest x1 11.3 us: expert_rows(): pre_act = jnp.dot(rows_in, w_gateup, preferred_element_type=F32)]
    gather x2, local copies, waits for them, and re-layouts: 4.7 us -> 10.8 us  [per_device(): flat_dx[slot_at]]
  transfers between devices with their start and end apart: 8 -> 5, of which waited for: 6 -> 3; matrix products, arithmetic and copies ran while one was open for 13% -> 6% of each run, Pallas kernels for 0% -> 61%
where the time goes in v1:
time: 325 us; the launch traced here: 324 us
  Pallas kernels  197 us (61%)
  local copies, waits for them, and re-layouts  35.5 us (11%)
  matrix products  34.8 us (11%)
  starting transfers between devices  19.3 us (6%)
  waiting for transfers between devices  18.6 us (6%)
  other arithmetic  17.2 us (5%)
    pallas_call x1, Pallas kernels, reduce_grads(): pl.pallas_call(functools.partial(grads_kernel, n, flight, ring_order(n)),...  197 us
    all_to_all x1, waiting for transfers between devices, per_device(): lax.all_to_all(send_in.reshape(flight, capacity, width), 'expert', split_...  13.7 us
    dot_general x1, matrix products, expert_rows(): pre_act = jnp.dot(rows_in, w_gateup, preferred_element_type=F32)  11.3 us
    gather x2, local copies, waits for them, and re-layouts, per_device(): flat_dx[slot_at]  10.8 us
    dot_general x1, matrix products, expert_rows(): lax.dot_general(pre_grad, w_gateup, (((1,), (1,)), ((), ())), preferred_e...  9.1 us
  transfers between devices with their start and end apart: 5, of which 3 were waited for; matrix products, arithmetic and copies ran while one was open for 6% of the time, Pallas kernels for 61%

profile of v1, /device:TPU:0, one launch (start us, length us, event | category | flops | bytes accessed | tf_op | source)
XLA Modules:
  0.0 323.5 jit_solution(17676375999232415825)
XLA Ops:
  5.3 2.4 scatter_custom_fusion.1
  7.8 2.4 scatter_custom_fusion
  13.1 1.5 broadcast_select_fusion
  14.7 4.4 %all-to-all-start.2 = ((bf16[4,64,2048]{2,1,0:T(8,128)(2,1)}), bf16[4,64,2048]{2,1,0:T(8,128)(2,1)S(1)}, u32[]{:S(2)}, u32[]{:S(2)}) async-start(bf16[4,64,2048]{2,1,0:T(8,128)(2,1)} %get-tuple-element.24), calls=%async_computation.2 | async-start | bytes 2097152 | tf_op jit(solution)/shard_map/all_to_all | solution.py:319
  19.8 13.7 %all-to-all-done.2 = bf16[4,64,2048]{2,1,0:T(8,128)(2,1)S(1)} async-done(((bf16[4,64,2048]{2,1,0:T(8,128)(2,1)}), bf16[4,64,2048]{2,1,0:T(8,128)(2,1)S(1)}, u32[]{:S(2)}, u32[]{:S(2)}) %all-to-all-start.2) | async-done | bytes 1048608 | tf_op jit(solution)/shard_map/all_to_all | solution.py:319
  33.5 3.7 %all-to-all-start.1 = ((bf16[4,64,2048]{2,1,0:T(8,128)(2,1)}), bf16[4,64,2048]{2,1,0:T(8,128)(2,1)S(1)}, u32[]{:S(2)}, u32[]{:S(2)}) async-start(bf16[4,64,2048]{2,1,0:T(8,128)(2,1)} %get-tuple-element.25), calls=%async_computation.1 | async-start | bytes 2097152 | tf_op jit(solution)/shard_map/all_to_all | solution.py:326
  37.2 11.3 %fusion.2 = f32[256,3072]{0,1:T(8,128)} fusion(bf16[256,2048]{1,0:T(8,128)(2,1)S(1)} %bitcast.79, bf16[1,2048,3072]{2,1,0:T(8,128)(2,1)} %param.12), kind=kOutput, calls=%fused_computation.9 | convolution fusion | flops 3221225472 | bytes 16777216 | tf_op jit(solution)/shard_map/dot_general | solution.py:255
  48.4 3.0 all-to-all-done.1
  51.4 5.7 %fusion.23 = f32[256]{0:T(256)S(1)} fusion(bf16[1,1536,2048]{2,1,0:T(8,128)(2,1)} %param.13, bf16[256,2048]{1,0:T(8,128)(2,1)S(1)} %bitcast.76, f32[256,3072]{0,1:T(8,128)} %fusion.2), kind=kOutput, calls=%fused_computation.32 | convolution fusion | flops 1615593216 | bytes 10486784 | tf_op jit(solution)/shard_map/dot_general | solution.py:260
  57.8 3.2 all-to-all-start.4
  61.0 3.2 fusion.46.ht_ref
  64.2 1.5 copy.83
  65.8 3.5 %gather_fusion.4 = f32[512]{0:T(512)S(1)} fusion(f32[256]{0:T(256)S(1)} %bitcast.75, s32[1024]{0:T(1024)S(1)} %pad_clamp_fusion), kind=kCustom, calls=%fused_computation.4 | custom fusion | bytes 6144 | tf_op jit(solution)/shard_map/gather | solution.py:370
  69.8 1.9 gather_fusion
  72.5 3.4 %all-to-all-start = ((bf16[4,64,2]{1,2,0:T(2,128)(2,1)}), bf16[4,64,2]{1,2,0:T(2,128)(2,1)S(1)}, u32[]{:S(2)}, u32[]{:S(2)}) async-start(bf16[4,64,2]{1,2,0:T(2,128)(2,1)} %copy.73), calls=%async_computation | async-start | bytes 4096 | tf_op jit(solution)/shard_map/all_to_all | solution.py:333
  77.6 2.0 all-to-all-done
  81.2 6.0 %multiply_convert_fusion.3 = (bf16[256,1536]{0,1:T(8,128)(2,1)S(1)}, bf16[256,1536]{0,1:T(8,128)(2,1)S(1)}) fusion(f32[256,3072]{0,1:T(8,128)} %fusion.2, bf16[256,2048]{1,0:T(8,128)(2,1)S(1)} %bitcast.81, bf16[1,1536,2048]{2,1,0:T(8,128)(2,1)} %param.13), kind=kOutput, calls=%fused_computation.29 | convolution fusion | flops 1615724544 | bytes 12058624 | tf_op jit(solution)/shard_map/dot_general | solution.py:261
  87.2 9.1 %fusion.17 = bf16[256,2048]{1,0:T(8,128)(2,1)} fusion(bf16[1,2048,3072]{2,1,0:T(8,128)(2,1)} %param.12, bf16[256,1536]{0,1:T(8,128)(2,1)S(1)} %get-tuple-element.17, bf16[256,1536]{0,1:T(8,128)(2,1)S(1)} %get-tuple-element.16), kind=kOutput, calls=%fused_computation.19 | convolution fusion | flops 3224895488 | bytes 15204352 | tf_op jit(solution)/shard_map/dot_general | solution.py:268
  97.6 2.6 copy.85.pg_ref
  100.2 4.5 %all-to-all-start.3 = ((bf16[4,64,2048]{2,1,0:T(8,128)(2,1)}), bf16[4,64,2048]{2,1,0:T(8,128)(2,1)}, u32[]{:S(2)}, u32[]{:S(2)}) async-start(bf16[4,64,2048]{2,1,0:T(8,128)(2,1)} %bitcast.82), calls=%async_computation.3 | async-start | bytes 2097152 | tf_op jit(solution)/shard_map/all_to_all | solution.py:353
  105.9 197.2 %grads.1 = (bf16[1,256,3072]{2,1,0:T(8,128)(2,1)}, bf16[1,192,2048]{2,1,0:T(8,128)(2,1)S(1)}, f32[2048,128]{1,0:T(8,128)S(1)}) custom-call(bf16[2048,256]{1,0:T(8,128)(2,1)S(1)} %bitcast.74, bf16[256,3072]{1,0:T(8,128)(2,1)} %copy.85.pg_ref, bf16[1536,256]{1,0:T(8,128)(2,1)S(1)} %copy-done.1, bf16[256,2048]{1,0:T(8,128)(2,1)} %fusion.21.dy_ref, ...), custom_call_target="tpu_custom_call" | custom-call | flops 4831838208 | bytes 2359296 | tf_op jit(solution)/shard_map/grads/pallas_call | solution.py:220
  303.1 6.6 %gather_fusion.3 = bf16[512,2048]{1,0:T(8,128)(2,1)} fusion(bf16[256,2048]{1,0:T(8,128)(2,1)} %bitcast.10, s32[1024]{0:T(1024)S(1)} %pad_clamp_fusion), kind=kCustom, calls=%fused_computation.3 | custom fusion | bytes 4196352 | tf_op jit(solution)/shard_map/gather | solution.py:371
  309.8 4.1 %gather.29 = bf16[128,4,2048]{2,1,0:T(4,128)(2,1)} reshape(bf16[512,2048]{1,0:T(8,128)(2,1)} %gather_fusion.3) | data formatting | bytes 4194304 | tf_op jit(solution)/shard_map/gather | solution.py:371
  313.9 5.5 %convert_reduce_fusion = f32[128,2048]{1,0:T(8,128)S(1)} fusion(bf16[128,4,2048]{2,1,0:T(4,128)(2,1)} %gather.29, pred[128,4]{1,0:T(8,128)(4,1)S(1)} %copy.66), kind=kLoop, calls=%fused_computation.15 | loop fusion | flops 2883584 | bytes 3146240 | tf_op jit(solution)/shard_map/reduce_sum | solution.py:381
  (84 shorter events, 20.1 us)
Async XLA Ops:
  0.6 9.7 %copy-start = (bf16[128,2048]{1,0:T(8,128)(2,1)S(1)}, bf16[128,2048]{1,0:T(8,128)(2,1)}, u32[]{:S(2)}) copy-start(bf16[128,2048]{1,0:T(8,128)(2,1)} %param.7) | copy-start | bytes 1572868
  10.4 1.4 copy-start.2
  14.6 4.4 %copy-start.4 = (bf16[2048,128]{1,0:T(8,128)(2,1)S(1)}, bf16[2048,128]{1,0:T(8,128)(2,1)}, u32[]{:S(2)}) copy-start(bf16[2048,128]{1,0:T(8,128)(2,1)} %param.10) | copy-start | bytes 1572868
  14.6 4.9 %copy-start.7 = (s32[128,4]{0,1:T(4,128)S(1)}, s32[128,4]{0,1:T(4,128)}, u32[]{:S(2)}) copy-start(s32[128,4]{0,1:T(4,128)} %param.11) | copy-start | bytes 6148
  14.7 5.2 %copy-start.8 = (f32[128]{0:T(128)S(1)}, f32[128]{0:T(128)}, u32[]{:S(2)}) copy-start(f32[128]{0:T(128)} %param.9) | copy-start | bytes 1540
  14.7 18.8 %all-to-all-start.2 = ((bf16[4,64,2048]{2,1,0:T(8,128)(2,1)}), bf16[4,64,2048]{2,1,0:T(8,128)(2,1)S(1)}, u32[]{:S(2)}, u32[]{:S(2)}) async-start(bf16[4,64,2048]{2,1,0:T(8,128)(2,1)} %get-tuple-element.24), calls=%async_computation.2 | async-start | bytes 2097152 | tf_op jit(solution)/shard_map/all_to_all | solution.py:319
  33.5 15.0 %copy-start.3 = (bf16[4,64,2048]{2,1,0:T(8,128)(2,1)}, bf16[4,64,2048]{2,1,0:T(8,128)(2,1)S(1)}, u32[]{:S(2)}) copy-start(bf16[4,64,2048]{2,1,0:T(8,128)(2,1)S(1)} %all-to-all-done.2) | copy-start | bytes 3145732
  33.5 17.9 %all-to-all-start.1 = ((bf16[4,64,2048]{2,1,0:T(8,128)(2,1)}), bf16[4,64,2048]{2,1,0:T(8,128)(2,1)S(1)}, u32[]{:S(2)}, u32[]{:S(2)}) async-start(bf16[4,64,2048]{2,1,0:T(8,128)(2,1)} %get-tuple-element.25), calls=%async_computation.1 | async-start | bytes 2097152 | tf_op jit(solution)/shard_map/all_to_all | solution.py:326
  57.8 7.9 %all-to-all-start.4 = ((bf16[4,64,2]{1,2,0:T(2,128)(2,1)}), bf16[4,64,2]{1,2,0:T(2,128)(2,1)S(1)}, u32[]{:S(2)}, u32[]{:S(2)}) async-start(bf16[4,64,2]{1,2,0:T(2,128)(2,1)} %copy.79), calls=%async_computation.4 | async-start | bytes 4096 | tf_op jit(solution)/shard_map/all_to_all | solution.py:360
  72.5 7.1 %all-to-all-start = ((bf16[4,64,2]{1,2,0:T(2,128)(2,1)}), bf16[4,64,2]{1,2,0:T(2,128)(2,1)S(1)}, u32[]{:S(2)}, u32[]{:S(2)}) async-start(bf16[4,64,2]{1,2,0:T(2,128)(2,1)} %copy.73), calls=%async_computation | async-start | bytes 4096 | tf_op jit(solution)/shard_map/all_to_all | solution.py:333
  100.2 202.9 %all-to-all-start.3 = ((bf16[4,64,2048]{2,1,0:T(8,128)(2,1)}), bf16[4,64,2048]{2,1,0:T(8,128)(2,1)}, u32[]{:S(2)}, u32[]{:S(2)}) async-start(bf16[4,64,2048]{2,1,0:T(8,128)(2,1)} %bitcast.82), calls=%async_computation.3 | async-start | bytes 2097152 | tf_op jit(solution)/shard_map/all_to_all | solution.py:353
  104.7 1.2 copy-start.1
  313.9 5.5 %copy-start.5 = (bf16[2048,128]{1,0:T(8,128)(2,1)S(1)}, bf16[2048,128]{1,0:T(8,128)(2,1)}, u32[]{:S(2)}) copy-start(bf16[2048,128]{1,0:T(8,128)(2,1)} %param.10) | copy-start | bytes 1572868
  319.4 2.1 copy-start.6

commit v2 on v1

--- a/solution.py
+++ b/solution.py
@@ -33,10 +33,11 @@
 
 def grads_kernel(
     copies, flight, order,
-    xt_ref, pg_ref, ht_ref, dy_ref, rp_ref,
-    gu_ref, dn_ref, rout_ref,
-    gu_buf, dn_buf, rx_e, rsum, rx_d, rfull,
+    xt_ref, pg_ref, ht_ref, dy_ref, score_ref, wg_hbm, tokt_ref, rw_ref, logit_ref, small_ref, ids_ref,
+    gu_ref, dn_ref, rout_ref, tg_ref,
+    gu_buf, dn_buf, rx_e, rsum, rx_d, rfull, rp_ref, wg_ref, back, home_dx, home_score, lg_ref,
     send_sem, recv_sem, es_send, es_recv, ds_send, ds_recv, dg_send, dg_recv, eg_send, eg_recv,
+    wg_sem, dx_send, dx_recv, sc_send, sc_recv,
 ):
     d = lax.axis_index("dp")
     e = lax.axis_index("expert")
@@ -47,6 +48,8 @@
     left = lookup(order, lax.rem(pos + n - 1, n))
     towards = (right, left)
 
+    load_w = pltpu.make_async_copy(wg_hbm, wg_ref, wg_sem)
+    load_w.start()
     barrier = pltpu.get_barrier_semaphore()
     for k in range(1, n):
         pl.semaphore_signal(barrier, inc=1, device_id=(lax.rem(d + k, n), e), device_id_type=MESH)
@@ -129,12 +132,54 @@
             device_id=(d, lax.rem(e + k, flight)), device_id_type=MESH,
         )
 
+    cap = home_dx.shape[1]
+
+    def block(ref, index):
+        return ref.at[pl.ds(pl.multiple_of(index * cap, cap), cap), :]
+
+    def give_score(k, source):
+        to = lax.rem(e + k, flight)
+        return pltpu.make_async_remote_copy(
+            src_ref=block(score_ref, to), dst_ref=home_score.at[source],
+            send_sem=sc_send.at[k - 1], recv_sem=sc_recv.at[k - 1],
+            device_id=(d, to), device_id_type=MESH,
+        )
+
+    def give_dx(k, source):
+        to = lax.rem(e + k, flight)
+        return pltpu.make_async_remote_copy(
+            src_ref=block(back, to), dst_ref=home_dx.at[source],
+            send_sem=dx_send.at[k - 1], recv_sem=dx_recv.at[k - 1],
+            device_id=(d, to), device_id_type=MESH,
+        )
+
+    def from_peer(k):
+        return lax.rem(e + flight - k, flight)
+
+    def one_hot(k):
+        spots = lax.broadcasted_iota(jnp.int32, (ids_ref.shape[0], flight * cap), 1)
+        return spots == ids_ref[:, top + k:top + k + 1]
+
+    top = ids_ref.shape[1] // 2
     for part in range(3):
         for way in range(2):
             slot(way, part, 0)[...] = own(way, part, owner_at(way, 0)).astype(BF16)
             hop(way, part, 0).start()
     for k in range(1, flight):
-        share_e(k).start()
+        give_score(k, e).start()
+    home_score[e] = score_ref[pl.ds(pl.multiple_of(e * cap, cap), cap), :]
+
+    load_w.wait()
+    width = back.shape[1]
+    tile = min(width, 512)
+    for col in range(0, width, tile):
+        back[:, col:col + tile] = lax.dot_general(
+            pg_ref[...], wg_ref[col:col + tile, :], (((1,), (1,)), ((), ())),
+            preferred_element_type=F32,
+        ).astype(BF16)
+    home_dx[e] = back[pl.ds(pl.multiple_of(e * cap, cap), cap), :]
+    for k in range(1, flight):
+        give_dx(k, e).start()
 
     def middle(step, carry):
         for part in range(3):
@@ -148,6 +193,34 @@
 
         @pl.when(step == 1)
         def _():
+            for k in range(1, flight):
+                give_score(k, from_peer(k)).wait_recv()
+            arrived = home_score[...].reshape(flight * cap, home_score.shape[2])
+            logits = logit_ref[...]
+            lanes = lax.broadcasted_iota(jnp.int32, logits.shape, 1)
+            scores = [
+                jnp.dot(
+                    one_hot(k).astype(F32), arrived,
+                    precision=lax.Precision.HIGHEST, preferred_element_type=F32,
+                )
+                for k in range(top)
+            ]
+            probs = [small_ref[:, k:k + 1] for k in range(top)]
+            mean = sum(p * q for p, q in zip(probs, scores))
+            z_weight = small_ref[:, top:top + 1]
+            log_total = small_ref[:, top + 1:top + 2]
+            grad = 2.0 * z_weight * log_total * jnp.exp(logits - log_total)
+            for k in range(top):
+                grad = grad + jnp.where(
+                    ids_ref[:, k:k + 1] == lanes, probs[k] * (scores[k] - mean), 0.0
+                )
+            lg_ref[...] = grad.astype(BF16)
+            rp_ref[...] = jnp.dot(tokt_ref[...], lg_ref[...], preferred_element_type=F32)
+            for k in range(1, flight):
+                share_e(k).start()
+
+        @pl.when(step == 2)
+        def _():
             total = rp_ref[pl.ds(pl.multiple_of(e * piece_e, piece_e), piece_e), :]
             for k in range(1, flight):
                 share_e(k).wait_recv()
@@ -156,7 +229,7 @@
             for k in range(1, n):
                 share_d(k).start()
 
-        @pl.when(step == 2)
+        @pl.when(step == 3)
         def _():
             total = rsum[pl.ds(pl.multiple_of(d * piece_d, piece_d), piece_d), :]
             for k in range(1, n):
@@ -166,19 +239,33 @@
             for k in range(1, n):
                 gather_d(k, d).start()
 
-        @pl.when(step == 3)
+        @pl.when(step == 4)
         def _():
             for k in range(1, n):
                 gather_d(k, lax.rem(d + n - k, n)).wait_recv()
             for k in range(1, flight):
                 gather_e(k, e).start()
 
+        @pl.when(step == 5)
+        def _():
+            for k in range(1, flight):
+                give_dx(k, from_peer(k)).wait_recv()
+            picks = sum(one_hot(k).astype(F32) for k in range(top)).astype(BF16)
+            rows = home_dx[...].reshape(flight * cap, width)
+            for col in range(0, width, tile):
+                total = jnp.dot(picks, rows[:, col:col + tile], preferred_element_type=F32)
+                total = total + lax.dot_general(
+                    lg_ref[...], rw_ref[col:col + tile, :], (((1,), (1,)), ((), ())),
+                    preferred_element_type=F32,
+                )
+                tg_ref[:, col:col + tile] = total.astype(BF16)
+
         return carry
 
     lax.fori_loop(1, n - 1, middle, 0)
 
     for k in range(1, flight):
-        gather_e(k, lax.rem(e + flight - k, flight)).wait_recv()
+        gather_e(k, from_peer(k)).wait_recv()
     rout_ref[...] = rfull[...]
     for part in range(3):
         for way in range(2):
@@ -204,13 +291,18 @@
     for k in range(1, flight):
         share_e(k).wait_send()
         gather_e(k, e).wait_send()
-
-
-def reduce_grads(copies, flight, xt, pre_grad, ht, dyk, router_part):
+        give_score(k, e).wait_send()
+        give_dx(k, e).wait_send()
+
+
+def reduce_grads(
+    copies, flight, xt, pre_grad, ht, dyk, score, w_gateup, tokt, router_weight, logits, small, ids
+):
     width, rows = xt.shape
     gate_up = pre_grad.shape[1]
     hidden = ht.shape[0]
-    routed = router_part.shape[1]
+    tok_count, routed = logits.shape
+    cap = rows // flight
     n = copies
     gu_rows, dn_rows = width // n, hidden // n
     piece_e = width // flight
@@ -223,9 +315,10 @@
             jax.ShapeDtypeStruct((1, gu_rows, gate_up), BF16),
             jax.ShapeDtypeStruct((1, dn_rows, width), BF16),
             jax.ShapeDtypeStruct((width, routed), F32),
-        ),
-        in_specs=[vmem] * 5,
-        out_specs=(vmem,) * 3,
+            jax.ShapeDtypeStruct((tok_count, width), BF16),
+        ),
+        in_specs=[vmem] * 5 + [pl.BlockSpec(memory_space=pl.ANY)] + [vmem] * 5,
+        out_specs=(vmem,) * 4,
         scratch_shapes=[
             pltpu.VMEM((2, 2, n, gu_rows // 2, gate_up // 2), BF16),
             pltpu.VMEM((2, n, dn_rows, width // 2), BF16),
@@ -233,14 +326,22 @@
             pltpu.VMEM((piece_e, routed), F32),
             pltpu.VMEM((n - 1, piece_d, routed), F32),
             pltpu.VMEM((width, routed), F32),
+            pltpu.VMEM((width, routed), F32),
+            pltpu.VMEM(w_gateup.shape, BF16),
+            pltpu.VMEM((rows, width), BF16),
+            pltpu.VMEM((flight, cap, width), BF16),
+            pltpu.VMEM((flight, cap, routed), F32),
+            pltpu.VMEM((tok_count, routed), BF16),
             dma((2, 3, n - 1)), dma((2, 3, n - 1)),
             dma((flight - 1,)), dma((flight - 1,)),
             dma((n - 1,)), dma((n - 1,)),
             dma((n - 1,)), dma((n - 1,)),
             dma((flight - 1,)), dma((flight - 1,)),
+            dma, dma((flight - 1,)), dma((flight - 1,)),
+            dma((flight - 1,)), dma((flight - 1,)),
         ],
         compiler_params=pltpu.CompilerParams(
-            collective_id=0, has_side_effects=True, vmem_limit_bytes=50 * 2**20
+            collective_id=0, has_side_effects=True, vmem_limit_bytes=58 * 2**20
         ),
         cost_estimate=pl.CostEstimate(
             flops=2 * rows * width * (gate_up + hidden),
@@ -248,27 +349,25 @@
             transcendentals=0,
         ),
         name="grads",
-    )(xt, pre_grad, ht, dyk, router_part)
-
-def expert_rows(rows_in, rows_grad, w_gateup, w_down):
+    )(xt, pre_grad, ht, dyk, score, w_gateup, tokt, router_weight, logits, small, ids)
+
+def expert_rows(rows_in, rows_raw, row_prob, w_gateup, w_down):
     hidden_units = w_down.shape[0]
     pre_act = jnp.dot(rows_in, w_gateup, preferred_element_type=F32)
     gate_pre = pre_act[:, :hidden_units]
     up_pre = pre_act[:, hidden_units:]
     activated = jax.nn.silu(gate_pre)
     hidden = (activated * up_pre).astype(BF16)
-    expert_out = jnp.dot(hidden, w_down, preferred_element_type=F32).astype(BF16)
-    hidden_grad = lax.dot_general(
-        rows_grad, w_down, (((1,), (1,)), ((), ())), preferred_element_type=F32
+    raw_grad = lax.dot_general(
+        rows_raw, w_down, (((1,), (1,)), ((), ())), preferred_element_type=F32
     )
+    score = jnp.sum(raw_grad * hidden.astype(F32), axis=1)
+    hidden_grad = row_prob[:, None] * raw_grad
     sigmoid_gate = jax.nn.sigmoid(gate_pre)
     gate_grad = hidden_grad * up_pre * sigmoid_gate * (1.0 + gate_pre * (1.0 - sigmoid_gate))
     up_grad = hidden_grad * activated
     pre_grad = jnp.concatenate([gate_grad, up_grad], axis=1).astype(BF16)
-    input_grad = lax.dot_general(
-        pre_grad, w_gateup, (((1,), (1,)), ((), ())), preferred_element_type=F32
-    ).astype(BF16)
-    return (hidden, pre_grad, expert_out, input_grad)
+    return (hidden, pre_grad, score)
 
 
 def split_pair(values):
@@ -345,49 +444,23 @@
     flat_raw = recv_raw.reshape(total_rows, width)
     row_prob = join_pair(recv_prob.reshape(total_rows, 2))
     flat_grad = (row_prob[:, None] * flat_raw.astype(jnp.float32)).astype(jnp.bfloat16)
-    hidden, pre_grad, produced, back_rows = expert_rows(flat_in, flat_grad, w_gateup, w_down)
-    slot_at = jnp.where(in_flight, position, 0)
-    row_score = jnp.sum(flat_raw.astype(jnp.float32) * produced.astype(jnp.float32), axis=1)
-    score_pair = split_pair(row_score)
-    home_dx, home_pair = (
-        lax.all_to_all(
-            back_rows.reshape(sources, capacity, width),
-            "expert",
-            split_axis=0,
-            concat_axis=0,
-            tiled=True,
-        ),
-        lax.all_to_all(
-            score_pair.reshape(sources, capacity, 2),
-            "expert",
-            split_axis=0,
-            concat_axis=0,
-            tiled=True,
-        ),
-    )
-    flat_dx = home_dx.reshape(flight * capacity, width)
-    flat_score = join_pair(home_pair.reshape(flight * capacity, 2))
-    scores = jnp.where(in_flight, flat_score[slot_at], 0.0).reshape(tok_count, top_count)
-    slot_dx = jnp.where(in_flight[:, None], flat_dx[slot_at], 0).reshape(
-        tok_count, top_count, width
-    )
-    mean_score = jnp.sum(probs * scores, axis=1, keepdims=True)
-    sel_grad = probs * (scores - mean_score)
-    z_grad = 2.0 * z_weight[:, None] * log_total[:, None] * jnp.exp(logits - log_total[:, None])
-    logit_grad = (z_grad + jnp.sum(jnp.where(choose, sel_grad[:, :, None], 0.0), axis=1)).astype(
-        jnp.bfloat16
-    )
-    token_grad = (
-        jnp.sum(slot_dx.astype(jnp.float32), axis=1)
-        + lax.dot_general(
-            logit_grad, router_weight, (((1,), (1,)), ((), ())), preferred_element_type=jnp.float32
-        )
-    ).astype(jnp.bfloat16)
-    router_part = lax.dot_general(
-        tokens, logit_grad, (((0,), (0,)), ((), ())), preferred_element_type=jnp.float32
-    )
-    gate_up_grad, down_grad, router_grad = reduce_grads(
-        lax.axis_size("dp"), flight, flat_in.T, pre_grad, hidden.T, flat_grad, router_part
+    hidden, pre_grad, score = expert_rows(flat_in, flat_raw, row_prob, w_gateup, w_down)
+    spot = jnp.where(in_flight, position, -1).reshape(tok_count, top_count)
+    small = jnp.concatenate([probs, z_weight[:, None], log_total[:, None]], axis=1)
+    gate_up_grad, down_grad, router_grad, token_grad = reduce_grads(
+        lax.axis_size("dp"),
+        flight,
+        flat_in.T,
+        pre_grad,
+        hidden.T,
+        flat_grad,
+        jnp.broadcast_to(score[:, None], (total_rows, routed)),
+        w_gateup,
+        tokens.T,
+        router_weight,
+        logits,
+        small,
+        jnp.concatenate([expert_ids, spot], axis=1),
     )
     return (token_grad, router_grad, gate_up_grad, down_grad)
 

time: 325 us -> 275 us (0.85)
  matrix products: 34.8 us -> 20.3 us
  local copies, waits for them, and re-layouts: 35.5 us -> 23.6 us
  other arithmetic: 17.2 us -> 6.63 us
  starting transfers between devices: 19.3 us -> 11.6 us
  waiting for transfers between devices: 18.6 us -> 13.4 us
    dot_general x5 -> x1, matrix products: 23.2 us -> 7.49 us  [expert_rows(): lax.dot_general(rows_raw, w_down, (((1,), (1,)), ((), ())), preferred_ele...]
    gather x5 -> x0, local copies, waits for them, and re-layouts: 14.4 us -> none  [the longest x2 10.8 us: per_device(): flat_dx[slot_at]]
    all_to_all x2 -> x0, starting transfers between devices: 7.75 us -> none  [the longest x1 4.53 us: per_device(): lax.all_to_all(back_rows.reshape(sources, capacity, width), 'expert', spl...]
    reduce_sum x3 -> x0, other arithmetic: 5.74 us -> none  [the longest x1 5.5 us: per_device(): jnp.sum(slot_dx.astype(jnp.float32), axis=1)]
    unnamed x22 -> x24, local copies, waits for them, and re-layouts: 3.82 us -> 7.45 us
  transfers between devices with their start and end apart: 5 -> 3, of which waited for: 3 -> 2; matrix products, arithmetic and copies ran while one was open for 6% -> 7% of each run, Pallas kernels for 61% -> 0%
where the time goes in v2:
time: 275 us; the launch traced here: 274 us
  Pallas kernels  198 us (72%)
  local copies, waits for them, and re-layouts  23.6 us (9%)
  matrix products  20.3 us (7%)
  waiting for transfers between devices  13.4 us (5%)
  starting transfers between devices  11.6 us (4%)
  other arithmetic  6.63 us (2%)
    pallas_call x1, Pallas kernels, reduce_grads(): pl.pallas_call(functools.partial(grads_kernel, n, flight, ring_order(n)),...  198 us
    all_to_all x1, waiting for transfers between devices, per_device(): lax.all_to_all(send_in.reshape(flight, capacity, width), 'expert', split_...  11.8 us
    dot_general x1, matrix products, expert_rows(): pre_act = jnp.dot(rows_in, w_gateup, preferred_element_type=F32)  11.3 us
    dot_general x1, matrix products, expert_rows(): lax.dot_general(rows_raw, w_down, (((1,), (1,)), ((), ())), preferred_ele...  7.49 us
    unnamed x24, local copies, waits for them, and re-layouts  7.45 us
  transfers between devices with their start and end apart: 3, of which 2 were waited for; matrix products, arithmetic and copies ran while one was open for 7% of the time, Pallas kernels for 0%

profile of v2, /device:TPU:0, one launch (start us, length us, event | category | flops | bytes accessed | tf_op | source)
XLA Modules:
  0.0 274.2 jit_solution(1805567659191962490)
XLA Ops:
  1.7 1.2 reduce-window.6
  3.9 2.4 scatter_custom_fusion.1
  6.3 1.6 exponential_reduce_fusion
  8.6 2.4 scatter_custom_fusion
  11.0 1.9 gather_fusion.1
  13.8 4.3 %all-to-all-start.1 = ((bf16[4,64,2]{1,2,0:T(2,128)(2,1)}), bf16[4,64,2]{1,2,0:T(2,128)(2,1)S(1)}, u32[]{:S(2)}, u32[]{:S(2)}) async-start(bf16[4,64,2]{1,2,0:T(2,128)(2,1)} %copy.89), calls=%async_computation.1 | async-start | bytes 4096 | tf_op jit(solution)/shard_map/all_to_all | solution.py:432
  18.1 1.4 gather_fusion
  19.5 1.4 gather_fusion.2
  20.9 1.5 broadcast_select_fusion
  22.4 3.6 %all-to-all-start = ((bf16[4,64,2048]{2,1,0:T(8,128)(2,1)}), bf16[4,64,2048]{2,1,0:T(8,128)(2,1)S(1)}, u32[]{:S(2)}, u32[]{:S(2)}) async-start(bf16[4,64,2048]{2,1,0:T(8,128)(2,1)} %get-tuple-element.24), calls=%async_computation | async-start | bytes 2097152 | tf_op jit(solution)/shard_map/all_to_all | solution.py:418
  26.0 1.0 copy.95
  28.6 11.8 %all-to-all-done = bf16[4,64,2048]{2,1,0:T(8,128)(2,1)S(1)} async-done(((bf16[4,64,2048]{2,1,0:T(8,128)(2,1)}), bf16[4,64,2048]{2,1,0:T(8,128)(2,1)S(1)}, u32[]{:S(2)}, u32[]{:S(2)}) %all-to-all-start) | async-done | bytes 1048608 | tf_op jit(solution)/shard_map/all_to_all | solution.py:418
  40.4 3.7 %all-to-all-start.2 = ((bf16[4,64,2048]{2,1,0:T(8,128)(2,1)}), bf16[4,64,2048]{2,1,0:T(8,128)(2,1)S(1)}, u32[]{:S(2)}, u32[]{:S(2)}) async-start(bf16[4,64,2048]{2,1,0:T(8,128)(2,1)} %get-tuple-element.23), calls=%async_computation.2 | async-start | bytes 2097152 | tf_op jit(solution)/shard_map/all_to_all | solution.py:425
  44.2 1.3 copy.86
  45.5 11.3 %fusion.11 = f32[256,3072]{0,1:T(8,128)} fusion(bf16[256,2048]{1,0:T(8,128)(2,1)S(1)} %bitcast.48, bf16[1,2048,3072]{2,1,0:T(8,128)(2,1)} %param.12), kind=kOutput, calls=%fused_computation.55 | convolution fusion | flops 3221225472 | bytes 16777216 | tf_op jit(solution)/shard_map/dot_general | solution.py:356
  56.8 1.6 all-to-all-done.2
  58.4 7.5 %multiply_reduce_fusion = (f32[256]{0:T(256)S(1)}, bf16[256,1536]{0,1:T(8,128)(2,1)}, bf16[256,1536]{0,1:T(8,128)(2,1)S(1)}, bf16[256,1536]{0,1:T(8,128)(2,1)S(1)}) fusion(f32[256,3072]{0,1:T(8,128)} %fusion.11, f32[256]{0:T(256)S(1)} %bitcast.54, bf16[256,2048]{1,0:T(8,128)(2,1)S(1)} %bitcast.49, bf16[1,1536,2048]{2,1,0:T(8,128)(2,1)} %param.13), kind=kOutput, calls=%fused_computation.9 | convolution fusion | flops 1618083584 | bytes 12847104 | tf_op jit(solution)/shard_map/dot_general | solution.py:361
  66.0 1.7 copy.97.pg_ref
  67.7 2.4 multiply_convert_fusion.dy_ref
  70.9 197.7 %grads.1 = (bf16[1,256,3072]{2,1,0:T(8,128)(2,1)}, bf16[1,192,2048]{2,1,0:T(8,128)(2,1)}, f32[2048,128]{1,0:T(8,128)}, bf16[128,2048]{1,0:T(8,128)(2,1)}) custom-call(bf16[2048,256]{1,0:T(8,128)(2,1)} %bitcast.46, bf16[256,3072]{1,0:T(8,128)(2,1)} %copy.97.pg_ref, bf16[1536,256]{1,0:T(8,128)(2,1)} %bitcast.51, ...), custom_call_target="tpu_custom_call" | custom-call | flops 4831838208 | bytes 2359296 | tf_op jit(solution)/shard_map/grads/pallas_call | solution.py:312
  268.6 2.0 copy.108
  270.7 1.0 copy.109
  271.6 1.1 copy.110
  273.3 0.9 copy.111
  (58 shorter events, 6.4 us)
Async XLA Ops:
  0.6 18.9 %copy-start = (bf16[128,2048]{1,0:T(8,128)(2,1)S(1)}, bf16[128,2048]{1,0:T(8,128)(2,1)}, u32[]{:S(2)}) copy-start(bf16[128,2048]{1,0:T(8,128)(2,1)} %param.8) | copy-start | bytes 1572868
  0.6 7.4 %copy-start.7 = (s32[128,4]{0,1:T(4,128)S(1)}, s32[128,4]{0,1:T(4,128)}, u32[]{:S(2)}) copy-start(s32[128,4]{0,1:T(4,128)} %param.11) | copy-start | bytes 6148
  1.6 16.5 %copy-start.1 = (bf16[128,2048]{1,0:T(8,128)(2,1)S(1)}, bf16[128,2048]{1,0:T(8,128)(2,1)}, u32[]{:S(2)}) copy-start(bf16[128,2048]{1,0:T(8,128)(2,1)} %param.7) | copy-start | bytes 1572868
  8.0 11.5 %copy-start.6 = (f32[128,128]{1,0:T(8,128)}, f32[128,128]{1,0:T(8,128)S(1)}, u32[]{:S(2)}) copy-start(f32[128,128]{1,0:T(8,128)S(1)} %copy.87.logit_ref) | copy-start | bytes 196612
  13.8 8.6 %all-to-all-start.1 = ((bf16[4,64,2]{1,2,0:T(2,128)(2,1)}), bf16[4,64,2]{1,2,0:T(2,128)(2,1)S(1)}, u32[]{:S(2)}, u32[]{:S(2)}) async-start(bf16[4,64,2]{1,2,0:T(2,128)(2,1)} %copy.89), calls=%async_computation.1 | async-start | bytes 4096 | tf_op jit(solution)/shard_map/all_to_all | solution.py:432
  22.4 4.7 %copy-start.8 = (f32[128]{0:T(128)S(1)}, f32[128]{0:T(128)}, u32[]{:S(2)}) copy-start(f32[128]{0:T(128)} %param.9) | copy-start | bytes 1540
  22.4 18.1 %all-to-all-start = ((bf16[4,64,2048]{2,1,0:T(8,128)(2,1)}), bf16[4,64,2048]{2,1,0:T(8,128)(2,1)S(1)}, u32[]{:S(2)}, u32[]{:S(2)}) async-start(bf16[4,64,2048]{2,1,0:T(8,128)(2,1)} %get-tuple-element.24), calls=%async_computation | async-start | bytes 2097152 | tf_op jit(solution)/shard_map/all_to_all | solution.py:418
  40.4 17.9 %all-to-all-start.2 = ((bf16[4,64,2048]{2,1,0:T(8,128)(2,1)}), bf16[4,64,2048]{2,1,0:T(8,128)(2,1)S(1)}, u32[]{:S(2)}, u32[]{:S(2)}) async-start(bf16[4,64,2048]{2,1,0:T(8,128)(2,1)} %get-tuple-element.23), calls=%async_computation.2 | async-start | bytes 2097152 | tf_op jit(solution)/shard_map/all_to_all | solution.py:425
  58.4 7.5 %copy-start.2 = (bf16[4,64,2048]{2,1,0:T(8,128)(2,1)}, bf16[4,64,2048]{2,1,0:T(8,128)(2,1)S(1)}, u32[]{:S(2)}) copy-start(bf16[4,64,2048]{2,1,0:T(8,128)(2,1)S(1)} %all-to-all-done.2) | copy-start | bytes 3145732
  268.6 2.1 copy-start.4
  268.6 3.0 %copy-start.3 = (bf16[1,256,3072]{2,1,0:T(8,128)(2,1)S(1)}, bf16[1,256,3072]{2,1,0:T(8,128)(2,1)}, u32[]{:S(2)}) copy-start(bf16[1,256,3072]{2,1,0:T(8,128)(2,1)} %get-tuple-element.35) | copy-start | bytes 4718596
  271.6 1.7 copy-start.5

commit v3 on v2

--- a/solution.py
+++ b/solution.py
@@ -33,7 +33,7 @@
 
 def grads_kernel(
     copies, flight, order,
-    xt_ref, pg_ref, ht_ref, dy_ref, score_ref, wg_hbm, tokt_ref, rw_ref, logit_ref, small_ref, ids_ref,
+    xt_ref, pg_ref, ht_ref, dy_ref, score_ref, wg_hbm, tokt_ref, rw_ref, logit_ref, small_ref, ids_ref, spot_ref, zw_ref,
     gu_ref, dn_ref, rout_ref, tg_ref,
     gu_buf, dn_buf, rx_e, rsum, rx_d, rfull, rp_ref, wg_ref, back, home_dx, home_score, lg_ref,
     send_sem, recv_sem, es_send, es_recv, ds_send, ds_recv, dg_send, dg_recv, eg_send, eg_recv,
@@ -158,9 +158,9 @@
 
     def one_hot(k):
         spots = lax.broadcasted_iota(jnp.int32, (ids_ref.shape[0], flight * cap), 1)
-        return spots == ids_ref[:, top + k:top + k + 1]
-
-    top = ids_ref.shape[1] // 2
+        return spots == spot_ref[:, k:k + 1]
+
+    top = ids_ref.shape[1]
     for part in range(3):
         for way in range(2):
             slot(way, part, 0)[...] = own(way, part, owner_at(way, 0)).astype(BF16)
@@ -207,8 +207,8 @@
             ]
             probs = [small_ref[:, k:k + 1] for k in range(top)]
             mean = sum(p * q for p, q in zip(probs, scores))
-            z_weight = small_ref[:, top:top + 1]
-            log_total = small_ref[:, top + 1:top + 2]
+            z_weight = zw_ref[...]
+            log_total = small_ref[:, top:top + 1]
             grad = 2.0 * z_weight * log_total * jnp.exp(logits - log_total)
             for k in range(top):
                 grad = grad + jnp.where(
@@ -296,7 +296,8 @@
 
 
 def reduce_grads(
-    copies, flight, xt, pre_grad, ht, dyk, score, w_gateup, tokt, router_weight, logits, small, ids
+    copies, flight, xt, pre_grad, ht, dyk, score, w_gateup, tokt, router_weight, logits, small, ids,
+    spot, zw,
 ):
     width, rows = xt.shape
     gate_up = pre_grad.shape[1]
@@ -317,7 +318,7 @@
             jax.ShapeDtypeStruct((width, routed), F32),
             jax.ShapeDtypeStruct((tok_count, width), BF16),
         ),
-        in_specs=[vmem] * 5 + [pl.BlockSpec(memory_space=pl.ANY)] + [vmem] * 5,
+        in_specs=[vmem] * 5 + [pl.BlockSpec(memory_space=pl.ANY)] + [vmem] * 7,
         out_specs=(vmem,) * 4,
         scratch_shapes=[
             pltpu.VMEM((2, 2, n, gu_rows // 2, gate_up // 2), BF16),
@@ -349,118 +350,241 @@
             transcendentals=0,
         ),
         name="grads",
-    )(xt, pre_grad, ht, dyk, score, w_gateup, tokt, router_weight, logits, small, ids)
-
-def expert_rows(rows_in, rows_raw, row_prob, w_gateup, w_down):
-    hidden_units = w_down.shape[0]
-    pre_act = jnp.dot(rows_in, w_gateup, preferred_element_type=F32)
-    gate_pre = pre_act[:, :hidden_units]
-    up_pre = pre_act[:, hidden_units:]
-    activated = jax.nn.silu(gate_pre)
-    hidden = (activated * up_pre).astype(BF16)
-    raw_grad = lax.dot_general(
-        rows_raw, w_down, (((1,), (1,)), ((), ())), preferred_element_type=F32
+    )(xt, pre_grad, ht, dyk, score, w_gateup, tokt, router_weight, logits, small, ids, spot, zw)
+
+def rows_kernel(
+    flight, cap,
+    tok_ref, og_ref, rw_ref, ids_ref, wg_hbm, wd_hbm,
+    xt_ref, ht_ref, pg_ref, dy_ref, score_ref, logit_ref, small_ref, spot_ref,
+    wg_ref, wd_ref, out_x, out_o, out_p, in_x, in_o, in_p, pre, hid,
+    wg_sem, wd_sem, x_send, x_recv, o_send, o_recv, p_send, p_recv,
+):
+    d = lax.axis_index("dp")
+    e = lax.axis_index("expert")
+    load_g = pltpu.make_async_copy(wg_hbm, wg_ref, wg_sem)
+    load_d = pltpu.make_async_copy(wd_hbm, wd_ref, wd_sem)
+    load_g.start()
+    load_d.start()
+    barrier = pltpu.get_barrier_semaphore()
+    for k in range(1, flight):
+        pl.semaphore_signal(barrier, inc=1, device_id=(d, lax.rem(e + k, flight)), device_id_type=MESH)
+
+    tok_count, top = ids_ref.shape
+    routed = rw_ref.shape[1]
+    hidden_units, width = wd_ref.shape
+    tile = min(hidden_units, 512)
+    pairs = flight // 2
+    lanes = lax.broadcasted_iota(jnp.int32, (tok_count, routed), 1)
+    choose = [ids_ref[:, k:k + 1] == lanes for k in range(top)]
+    member = sum(c.astype(F32) for c in choose)
+    earlier = lax.broadcasted_iota(jnp.int32, (tok_count, tok_count), 0) > (
+        lax.broadcasted_iota(jnp.int32, (tok_count, tok_count), 1)
     )
-    score = jnp.sum(raw_grad * hidden.astype(F32), axis=1)
-    hidden_grad = row_prob[:, None] * raw_grad
-    sigmoid_gate = jax.nn.sigmoid(gate_pre)
-    gate_grad = hidden_grad * up_pre * sigmoid_gate * (1.0 + gate_pre * (1.0 - sigmoid_gate))
-    up_grad = hidden_grad * activated
-    pre_grad = jnp.concatenate([gate_grad, up_grad], axis=1).astype(BF16)
-    return (hidden, pre_grad, score)
-
-
-def split_pair(values):
-    upper = values.astype(jnp.bfloat16)
-    lower = (values - upper.astype(jnp.float32)).astype(jnp.bfloat16)
-    return jnp.stack([upper, lower], axis=-1)
-
-
-def join_pair(pair):
-    return pair[..., 0].astype(jnp.float32) + pair[..., 1].astype(jnp.float32)
+    rank = jnp.dot(earlier.astype(F32).astype(BF16), member.astype(BF16), preferred_element_type=F32)
+    rank = jnp.where(member > 0.0, rank, -1.0)
+    by_expert = rank.T.astype(jnp.int32)
+    ranks = lax.broadcasted_iota(jnp.int32, (cap, tok_count), 0)
+    picks = [by_expert[f:f + 1, :] == ranks for f in range(flight)]
+
+    pl.semaphore_wait(barrier, flight - 1)
+
+    def rows_of(index):
+        return pl.ds(pl.multiple_of(index * cap, cap), cap)
+
+    def peers():
+        found = []
+        for i in range(1, pairs):
+            pair = lax.rem(lax.div(e, 2) + i, pairs)
+            found += [pair * 2 + lax.rem(e, 2), pair * 2 + 1 - lax.rem(e, 2)]
+        return found + [lax.div(e, 2) * 2 + 1 - lax.rem(e, 2)]
+
+    def give(out, into, sends, recvs, source, target):
+        return pltpu.make_async_remote_copy(
+            src_ref=out.at[rows_of(target), :], dst_ref=into.at[rows_of(source), :],
+            send_sem=sends.at[target], recv_sem=recvs.at[source],
+            device_id=(d, target), device_id_type=MESH,
+        )
+
+    give_x = functools.partial(give, out_x, in_x, x_send, x_recv)
+    give_o = functools.partial(give, out_o, in_o, o_send, o_recv)
+    give_p = functools.partial(give, out_p, in_p, p_send, p_recv)
+
+    for f in range(flight):
+        out_x[f * cap:(f + 1) * cap, :] = jnp.dot(
+            picks[f].astype(F32).astype(BF16), tok_ref[...], preferred_element_type=F32
+        ).astype(BF16)
+    for to in peers():
+        give_x(e, to).start()
+    for f in range(flight):
+        out_o[f * cap:(f + 1) * cap, :] = jnp.dot(
+            picks[f].astype(F32).astype(BF16), og_ref[...], preferred_element_type=F32
+        ).astype(BF16)
+    for to in peers():
+        give_o(e, to).start()
+
+    logits = jnp.dot(tok_ref[...], rw_ref[...], preferred_element_type=F32)
+    logit_ref[...] = logits
+    chosen = [
+        jnp.exp(jnp.sum(jnp.where(c, logits, 0.0), axis=1, keepdims=True)) for c in choose
+    ]
+    norm = sum(chosen)
+    probs = [c / norm for c in chosen]
+    log_total = jnp.log(jnp.sum(jnp.exp(logits), axis=1, keepdims=True))
+    small = jnp.where(lanes == top, log_total, 0.0)
+    spot = jnp.full(lanes.shape, -1, jnp.int32)
+    weight = jnp.zeros(lanes.shape, F32)
+    place = jnp.where((rank >= 0.0) & (lanes < flight), rank + (lanes * cap).astype(F32) + 1.0, 0.0)
+    for k in range(top):
+        small = jnp.where(lanes == k, probs[k], small)
+        at = jnp.sum(jnp.where(choose[k], place, 0.0), axis=1, keepdims=True) - 1.0
+        spot = jnp.where(lanes == k, at.astype(jnp.int32), spot)
+        weight = weight + jnp.where(choose[k], probs[k], 0.0)
+    small_ref[...] = small
+    spot_ref[...] = spot
+    weight = weight.T
+    for f in range(flight):
+        row = jnp.sum(jnp.where(picks[f], weight[f:f + 1, :], 0.0), axis=1, keepdims=True)
+        out_p[f * cap:(f + 1) * cap, :] = jnp.broadcast_to(row, (cap, routed))
+    for to in peers():
+        give_p(e, to).start()
+    in_x[rows_of(e), :] = out_x[rows_of(e), :]
+    in_o[rows_of(e), :] = out_o[rows_of(e), :]
+    in_p[rows_of(e), :] = out_p[rows_of(e), :]
+
+    def arrived(gives, pair):
+        for core in range(2):
+            source = pair * 2 + core
+
+            @pl.when(source != e)
+            def _():
+                for g in gives:
+                    g(source, e).wait_recv()
+
+    def pair_rows(pair):
+        return pl.ds(pl.multiple_of(pair * (2 * cap), 2 * cap), 2 * cap)
+
+    load_g.wait()
+
+    def forward(i, carry):
+        pair = lax.rem(lax.div(e, 2) + i, pairs)
+        arrived([give_x], pair)
+        rows = pair_rows(pair)
+        for col in range(0, 2 * hidden_units, tile):
+            pre[rows, col:col + tile] = jnp.dot(
+                in_x[rows, :], wg_ref[:, col:col + tile], preferred_element_type=F32
+            )
+        return carry
+
+    lax.fori_loop(0, pairs, forward, 0)
+    load_d.wait()
+
+    def backward(i, carry):
+        pair = lax.rem(lax.div(e, 2) + i, pairs)
+        arrived([give_o, give_p], pair)
+        rows = pair_rows(pair)
+        prob = in_p[rows, 0:1]
+        score = jnp.zeros((2 * cap, 1), F32)
+        for col in range(0, hidden_units, tile):
+            raw = lax.dot_general(
+                in_o[rows, :], wd_ref[col:col + tile, :], (((1,), (1,)), ((), ())),
+                preferred_element_type=F32,
+            )
+            gate = pre[rows, col:col + tile]
+            up = pre[rows, hidden_units + col:hidden_units + col + tile]
+            sig = jax.nn.sigmoid(gate)
+            active = gate * sig
+            hidden = (active * up).astype(BF16)
+            hid[rows, col:col + tile] = hidden
+            score = score + jnp.sum(raw * hidden.astype(F32), axis=1, keepdims=True)
+            grad = prob * raw
+            pg_ref[rows, col:col + tile] = (
+                grad * up * sig * (1.0 + gate * (1.0 - sig))
+            ).astype(BF16)
+            pg_ref[rows, hidden_units + col:hidden_units + col + tile] = (grad * active).astype(BF16)
+        score_ref[rows, :] = jnp.broadcast_to(score, (2 * cap, routed))
+        dy_ref[rows, :] = (prob * in_o[rows, :].astype(F32)).astype(BF16)
+        return carry
+
+    xt_ref[...] = in_x[...].T
+    lax.fori_loop(0, pairs, backward, 0)
+    ht_ref[...] = hid[...].T
+    for to in peers():
+        give_x(e, to).wait_send()
+        give_o(e, to).wait_send()
+        give_p(e, to).wait_send()
+
+
+def expert_rows(flight, tokens, out_grad, router_weight, ids, w_gateup, w_down):
+    tok_count, width = tokens.shape
+    routed = router_weight.shape[1]
+    hidden = w_down.shape[0]
+    cap = tok_count // 2
+    rows = flight * cap
+    dma = pltpu.SemaphoreType.DMA
+    vmem = pl.BlockSpec(memory_space=pltpu.VMEM)
+    hbm = pl.BlockSpec(memory_space=pl.ANY)
+    shape = jax.ShapeDtypeStruct
+    return pl.pallas_call(
+        functools.partial(rows_kernel, flight, cap),
+        out_shape=(
+            shape((width, rows), BF16),
+            shape((hidden, rows), BF16),
+            shape((rows, 2 * hidden), BF16),
+            shape((rows, width), BF16),
+            shape((rows, routed), F32),
+            shape((tok_count, routed), F32),
+            shape((tok_count, routed), F32),
+            shape((tok_count, routed), jnp.int32),
+        ),
+        in_specs=[vmem] * 4 + [hbm] * 2,
+        out_specs=(vmem,) * 8,
+        scratch_shapes=[
+            pltpu.VMEM(w_gateup.shape, BF16),
+            pltpu.VMEM(w_down.shape, BF16),
+            pltpu.VMEM((rows, width), BF16),
+            pltpu.VMEM((rows, width), BF16),
+            pltpu.VMEM((rows, routed), F32),
+            pltpu.VMEM((rows, width), BF16),
+            pltpu.VMEM((rows, width), BF16),
+            pltpu.VMEM((rows, routed), F32),
+            pltpu.VMEM((rows, 2 * hidden), F32),
+            pltpu.VMEM((rows, hidden), BF16),
+            dma, dma,
+        ] + [dma((flight,))] * 6,
+        compiler_params=pltpu.CompilerParams(
+            collective_id=1, has_side_effects=True, vmem_limit_bytes=58 * 2**20
+        ),
+        cost_estimate=pl.CostEstimate(
+            flops=6 * rows * width * hidden,
+            bytes_accessed=6 * width * hidden,
+            transcendentals=rows * hidden,
+        ),
+        name="rows",
+    )(tokens, out_grad, router_weight, ids, w_gateup, w_down)
 
 
 def per_device(tokens, out_grad, z_weight, router_weight, expert_ids, gate_up_weight, down_weight):
-    tok_count, width = tokens.shape
-    top_count = expert_ids.shape[1]
-    routed = router_weight.shape[1]
     flight = lax.axis_size("expert")
-    capacity = tok_count // 2
     w_gateup = gate_up_weight[0]
-    w_down = down_weight[0]
-    hidden_units = w_down.shape[0]
-    logits = jnp.dot(tokens, router_weight, preferred_element_type=jnp.float32)
-    choose = expert_ids[:, :, None] == jnp.arange(routed, dtype=jnp.int32)[None, None, :]
-    selected = jnp.sum(jnp.where(choose, logits[:, None, :], 0.0), axis=2)
-    sel_exp = jnp.exp(selected)
-    probs = sel_exp / jnp.sum(sel_exp, axis=1, keepdims=True)
-    log_total = jnp.log(jnp.sum(jnp.exp(logits), axis=1))
-    flat_ids = expert_ids.reshape(-1)
-    slot_count = tok_count * top_count
-    member = (flat_ids[:, None] == jnp.arange(flight, dtype=jnp.int32)[None, :]).astype(jnp.int32)
-    ranks = jnp.sum((jnp.cumsum(member, axis=0) - 1) * member, axis=1)
-    in_flight = flat_ids < flight
-    position = jnp.where(in_flight, flat_ids * capacity + ranks, flight * capacity)
-    source_slot = (
-        jnp.zeros((flight * capacity,), jnp.int32)
-        .at[position]
-        .set(jnp.arange(slot_count, dtype=jnp.int32), mode="drop")
+    xt, ht, pre_grad, dyk, score, logits, small, spot = expert_rows(
+        flight, tokens, out_grad, router_weight, expert_ids, w_gateup, down_weight[0]
     )
-    filled = jnp.zeros((flight * capacity,), jnp.bool_).at[position].set(True, mode="drop")
-    source_tok = source_slot // top_count
-    send_in = jnp.where(filled[:, None], tokens[source_tok], 0)
-    slot_prob = jnp.where(filled, probs.reshape(-1)[source_slot], 0.0)
-    counts = jnp.sum(member, axis=0)
-    count_msg = jnp.stack([counts // 128, counts % 128], axis=1).astype(jnp.bfloat16)
-    send_raw = jnp.where(filled[:, None], out_grad[source_tok], 0)
-    prob_pair = split_pair(slot_prob)
-    recv_in, recv_raw, recv_prob, recv_counts = (
-        lax.all_to_all(
-            send_in.reshape(flight, capacity, width),
-            "expert",
-            split_axis=0,
-            concat_axis=0,
-            tiled=True,
-        ),
-        lax.all_to_all(
-            send_raw.reshape(flight, capacity, width),
-            "expert",
-            split_axis=0,
-            concat_axis=0,
-            tiled=True,
-        ),
-        lax.all_to_all(
-            prob_pair.reshape(flight, capacity, 2),
-            "expert",
-            split_axis=0,
-            concat_axis=0,
-            tiled=True,
-        ),
-        lax.all_to_all(count_msg, "expert", split_axis=0, concat_axis=0, tiled=True),
-    )
-    sources = recv_in.shape[0]
-    total_rows = sources * capacity
-    flat_in = recv_in.reshape(total_rows, width)
-    flat_raw = recv_raw.reshape(total_rows, width)
-    row_prob = join_pair(recv_prob.reshape(total_rows, 2))
-    flat_grad = (row_prob[:, None] * flat_raw.astype(jnp.float32)).astype(jnp.bfloat16)
-    hidden, pre_grad, score = expert_rows(flat_in, flat_raw, row_prob, w_gateup, w_down)
-    spot = jnp.where(in_flight, position, -1).reshape(tok_count, top_count)
-    small = jnp.concatenate([probs, z_weight[:, None], log_total[:, None]], axis=1)
     gate_up_grad, down_grad, router_grad, token_grad = reduce_grads(
         lax.axis_size("dp"),
         flight,
-        flat_in.T,
+        xt,
         pre_grad,
-        hidden.T,
-        flat_grad,
-        jnp.broadcast_to(score[:, None], (total_rows, routed)),
+        ht,
+        dyk,
+        score,
         w_gateup,
         tokens.T,
         router_weight,
         logits,
         small,
-        jnp.concatenate([expert_ids, spot], axis=1),
+        expert_ids,
+        spot,
+        z_weight[:, None],
     )
     return (token_grad, router_grad, gate_up_grad, down_grad)
 

time: 275 us -> 245 us (0.89)
  Pallas kernels: 198 us -> 233 us
  matrix products: 20.3 us -> 0 us
  waiting for transfers between devices: 13.4 us -> 0 us
  local copies, waits for them, and re-layouts: 23.6 us -> 10.4 us
  starting transfers between devices: 11.6 us -> 0 us
  other arithmetic: 6.63 us -> 0 us
    pallas_call x0 -> x1, Pallas kernels: none -> 34.8 us  [expert_rows(): pl.pallas_call(functools.partial(rows_kernel, flight, cap), out_shape=(sh...]
    dot_general x3 -> x0, matrix products: 20.3 us -> none  [the longest x1 11.3 us: expert_rows(): pre_act = jnp.dot(rows_in, w_gateup, preferred_element_type=F32)]
    all_to_all x3 -> x0, waiting for transfers between devices: 13.4 us -> none  [the longest x1 11.8 us: per_device(): lax.all_to_all(send_in.reshape(flight, capacity, width), 'expert', split_...]
    all_to_all x3 -> x0, starting transfers between devices: 11.6 us -> none  [the longest x1 4.26 us: per_device(): lax.all_to_all(prob_pair.reshape(flight, capacity, 2), 'expert', split_ax...]
    scatter x2 -> x0, local copies, waits for them, and re-layouts: 4.88 us -> none  [the longest x1 2.45 us: per_device(): jnp.zeros((flight * capacity,), jnp.bool_).at[position]]
    gather x3 -> x0, local copies, waits for them, and re-layouts: 4.66 us -> none  [the longest x1 1.95 us: per_device(): slot_prob = jnp.where(filled, probs.reshape(-1)[source_slot], 0.0)]
    unnamed x24 -> x12, local copies, waits for them, and re-layouts: 7.45 us -> 9.02 us
  transfers between devices with their start and end apart: 3 -> 0, of which waited for: 2 -> 0; matrix products, arithmetic and copies ran while one was open for 7% -> 0% of each run, Pallas kernels for 0% -> 0%
where the time goes in v3:
time: 245 us; the launch traced here: 244 us
  Pallas kernels  233 us (95%)
  local copies, waits for them, and re-layouts  10.4 us (4%)
    pallas_call x1, Pallas kernels, reduce_grads(): pl.pallas_call(functools.partial(grads_kernel, n, flight, ring_order(n)),...  198 us
    pallas_call x1, Pallas kernels, expert_rows(): pl.pallas_call(functools.partial(rows_kernel, flight, cap), out_shape=(sh...  34.8 us
    unnamed x12, local copies, waits for them, and re-layouts  9.02 us

profile of v3, /device:TPU:0, one launch (start us, length us, event | category | flops | bytes accessed | tf_op | source)
XLA Modules:
  0.0 244.0 jit_solution(8291503359612882549)
XLA Ops:
  0.6 1.4 copy.11.ids_ref
  2.0 1.4 copy.14.zw_ref
  3.4 2.0 copy.12
  5.5 34.8 %rows.1 = (bf16[2048,256]{1,0:T(8,128)(2,1)}, bf16[1536,256]{1,0:T(8,128)(2,1)}, bf16[256,3072]{1,0:T(8,128)(2,1)}, bf16[256,2048]{1,0:T(8,128)(2,1)}, f32[256,1...) custom-call(bf16[128,2048]{1,0:T(8,128)(2,1)} %tok_ref.1, bf16[128,2048]{1,0:T(8,128)(2,1)} %og_ref.1, ...), custom_call_target="tpu_custom_call" | custom-call | flops 4831838208 | bytes 18874368 | tf_op jit(solution)/shard_map/rows/pallas_call | solution.py:527
  40.3 198.1 %grads.1 = (bf16[1,256,3072]{2,1,0:T(8,128)(2,1)}, bf16[1,192,2048]{2,1,0:T(8,128)(2,1)}, f32[2048,128]{1,0:T(8,128)}, bf16[128,2048]{1,0:T(8,128)(2,1)}) custom-call(bf16[2048,256]{1,0:T(8,128)(2,1)} %get-tuple-element.16.xt_ref, bf16[256,3072]{1,0:T(8,128)(2,1)} %get-tuple-element.17.pg_ref, bf16[1536,256]{1,0:T(8,128)(2,1)} %get-tuple-element.18.ht_ref, ...), custom_call_target="tpu_custom_call" | custom-call | flops 4831838208 | bytes 2359296 | tf_op jit(solution)/shard_map/grads/pallas_call | solution.py:313
  238.4 0.0 copy-start.1
  238.5 0.0 copy-start
  238.5 2.0 copy.19
  240.5 0.0 copy-done.1
  240.5 1.0 copy.20
  241.5 0.0 copy-done
  241.5 0.0 copy-start.2
  241.5 1.1 copy.21
  242.6 0.5 copy-done.2
  243.2 0.9 copy.22
Async XLA Ops:
  238.4 2.1 copy-start.1
  238.5 3.0 %copy-start = (bf16[1,256,3072]{2,1,0:T(8,128)(2,1)S(1)}, bf16[1,256,3072]{2,1,0:T(8,128)(2,1)}, u32[]{:S(2)}) copy-start(bf16[1,256,3072]{2,1,0:T(8,128)(2,1)} %get-tuple-element.34) | copy-start | bytes 4718596
  241.5 1.7 copy-start.2

commit v4 on v3

--- a/solution.py
+++ b/solution.py
@@ -31,13 +31,13 @@
     return value
 
 
-def grads_kernel(
-    copies, flight, order,
-    xt_ref, pg_ref, ht_ref, dy_ref, score_ref, wg_hbm, tokt_ref, rw_ref, logit_ref, small_ref, ids_ref, spot_ref, zw_ref,
+def grads_part(
+    copies, flight, order, top,
+    tok_ref, rw_ref, wg_ref, xt_ref, pg_ref, ht_ref, dy_ref, score_ref, logit_ref, small_ref, spot_ref, back, home_dx,
     gu_ref, dn_ref, rout_ref, tg_ref,
-    gu_buf, dn_buf, rx_e, rsum, rx_d, rfull, rp_ref, wg_ref, back, home_dx, home_score, lg_ref,
+    gu_buf, dn_buf, rx_e, rsum, rx_d, rfull, rp_ref, home_score, lg_ref,
     send_sem, recv_sem, es_send, es_recv, ds_send, ds_recv, dg_send, dg_recv, eg_send, eg_recv,
-    wg_sem, dx_send, dx_recv, sc_send, sc_recv,
+    dx_send, dx_recv, sc_send, sc_recv,
 ):
     d = lax.axis_index("dp")
     e = lax.axis_index("expert")
@@ -47,15 +47,6 @@
     right = lookup(order, lax.rem(pos + 1, n))
     left = lookup(order, lax.rem(pos + n - 1, n))
     towards = (right, left)
-
-    load_w = pltpu.make_async_copy(wg_hbm, wg_ref, wg_sem)
-    load_w.start()
-    barrier = pltpu.get_barrier_semaphore()
-    for k in range(1, n):
-        pl.semaphore_signal(barrier, inc=1, device_id=(lax.rem(d + k, n), e), device_id_type=MESH)
-    for k in range(1, flight):
-        pl.semaphore_signal(barrier, inc=1, device_id=(d, lax.rem(e + k, flight)), device_id_type=MESH)
-    pl.semaphore_wait(barrier, n + flight - 2)
 
     gu_rows = gu_ref.shape[1]
     half_rows = gu_rows // 2
@@ -132,7 +123,7 @@
             device_id=(d, lax.rem(e + k, flight)), device_id_type=MESH,
         )
 
-    cap = home_dx.shape[1]
+    cap = home_score.shape[1]
 
     def block(ref, index):
         return ref.at[pl.ds(pl.multiple_of(index * cap, cap), cap), :]
@@ -148,7 +139,7 @@
     def give_dx(k, source):
         to = lax.rem(e + k, flight)
         return pltpu.make_async_remote_copy(
-            src_ref=block(back, to), dst_ref=home_dx.at[source],
+            src_ref=block(back, to), dst_ref=block(home_dx, source),
             send_sem=dx_send.at[k - 1], recv_sem=dx_recv.at[k - 1],
             device_id=(d, to), device_id_type=MESH,
         )
@@ -157,10 +148,9 @@
         return lax.rem(e + flight - k, flight)
 
     def one_hot(k):
-        spots = lax.broadcasted_iota(jnp.int32, (ids_ref.shape[0], flight * cap), 1)
+        spots = lax.broadcasted_iota(jnp.int32, (tok_ref.shape[0], flight * cap), 1)
         return spots == spot_ref[:, k:k + 1]
 
-    top = ids_ref.shape[1]
     for part in range(3):
         for way in range(2):
             slot(way, part, 0)[...] = own(way, part, owner_at(way, 0)).astype(BF16)
@@ -169,7 +159,6 @@
         give_score(k, e).start()
     home_score[e] = score_ref[pl.ds(pl.multiple_of(e * cap, cap), cap), :]
 
-    load_w.wait()
     width = back.shape[1]
     tile = min(width, 512)
     for col in range(0, width, tile):
@@ -177,9 +166,8 @@
             pg_ref[...], wg_ref[col:col + tile, :], (((1,), (1,)), ((), ())),
             preferred_element_type=F32,
         ).astype(BF16)
-    home_dx[e] = back[pl.ds(pl.multiple_of(e * cap, cap), cap), :]
-    for k in range(1, flight):
-        give_dx(k, e).start()
+    own_rows = pl.ds(pl.multiple_of(e * cap, cap), cap)
+    home_dx[own_rows, :] = back[own_rows, :]
 
     def middle(step, carry):
         for part in range(3):
@@ -195,6 +183,8 @@
         def _():
             for k in range(1, flight):
                 give_score(k, from_peer(k)).wait_recv()
+            for k in range(1, flight):
+                give_dx(k, e).start()
             arrived = home_score[...].reshape(flight * cap, home_score.shape[2])
             logits = logit_ref[...]
             lanes = lax.broadcasted_iota(jnp.int32, logits.shape, 1)
@@ -207,15 +197,15 @@
             ]
             probs = [small_ref[:, k:k + 1] for k in range(top)]
             mean = sum(p * q for p, q in zip(probs, scores))
-            z_weight = zw_ref[...]
+            z_weight = small_ref[:, top + 1:top + 2]
             log_total = small_ref[:, top:top + 1]
             grad = 2.0 * z_weight * log_total * jnp.exp(logits - log_total)
             for k in range(top):
                 grad = grad + jnp.where(
-                    ids_ref[:, k:k + 1] == lanes, probs[k] * (scores[k] - mean), 0.0
+                    spot_ref[:, top + k:top + k + 1] == lanes, probs[k] * (scores[k] - mean), 0.0
                 )
             lg_ref[...] = grad.astype(BF16)
-            rp_ref[...] = jnp.dot(tokt_ref[...], lg_ref[...], preferred_element_type=F32)
+            rp_ref[...] = jnp.dot(tok_ref[...].T, lg_ref[...], preferred_element_type=F32)
             for k in range(1, flight):
                 share_e(k).start()
 
@@ -225,17 +215,19 @@
             for k in range(1, flight):
                 share_e(k).wait_recv()
                 total = total + rx_e[k - 1]
-            rsum[...] = total
+            rp_ref[pl.ds(pl.multiple_of(e * piece_e, piece_e), piece_e), :] = total
+            rsum[...] = total.astype(BF16)
             for k in range(1, n):
                 share_d(k).start()
 
         @pl.when(step == 3)
         def _():
-            total = rsum[pl.ds(pl.multiple_of(d * piece_d, piece_d), piece_d), :]
+            mine = pl.ds(pl.multiple_of(e * piece_e + d * piece_d, piece_d), piece_d)
+            total = rp_ref[mine, :]
             for k in range(1, n):
                 share_d(k).wait_recv()
-                total = total + rx_d[k - 1]
-            rfull[pl.ds(pl.multiple_of(e * piece_e + d * piece_d, piece_d), piece_d), :] = total
+                total = total + rx_d[k - 1].astype(F32)
+            rfull[mine, :] = total
             for k in range(1, n):
                 gather_d(k, d).start()
 
@@ -251,7 +243,7 @@
             for k in range(1, flight):
                 give_dx(k, from_peer(k)).wait_recv()
             picks = sum(one_hot(k).astype(F32) for k in range(top)).astype(BF16)
-            rows = home_dx[...].reshape(flight * cap, width)
+            rows = home_dx[...]
             for col in range(0, width, tile):
                 total = jnp.dot(picks, rows[:, col:col + tile], preferred_element_type=F32)
                 total = total + lax.dot_general(
@@ -295,87 +287,26 @@
         give_dx(k, e).wait_send()
 
 
-def reduce_grads(
-    copies, flight, xt, pre_grad, ht, dyk, score, w_gateup, tokt, router_weight, logits, small, ids,
-    spot, zw,
-):
-    width, rows = xt.shape
-    gate_up = pre_grad.shape[1]
-    hidden = ht.shape[0]
-    tok_count, routed = logits.shape
-    cap = rows // flight
-    n = copies
-    gu_rows, dn_rows = width // n, hidden // n
-    piece_e = width // flight
-    piece_d = piece_e // n
-    dma = pltpu.SemaphoreType.DMA
-    vmem = pl.BlockSpec(memory_space=pltpu.VMEM)
-    return pl.pallas_call(
-        functools.partial(grads_kernel, n, flight, ring_order(n)),
-        out_shape=(
-            jax.ShapeDtypeStruct((1, gu_rows, gate_up), BF16),
-            jax.ShapeDtypeStruct((1, dn_rows, width), BF16),
-            jax.ShapeDtypeStruct((width, routed), F32),
-            jax.ShapeDtypeStruct((tok_count, width), BF16),
-        ),
-        in_specs=[vmem] * 5 + [pl.BlockSpec(memory_space=pl.ANY)] + [vmem] * 7,
-        out_specs=(vmem,) * 4,
-        scratch_shapes=[
-            pltpu.VMEM((2, 2, n, gu_rows // 2, gate_up // 2), BF16),
-            pltpu.VMEM((2, n, dn_rows, width // 2), BF16),
-            pltpu.VMEM((flight - 1, piece_e, routed), F32),
-            pltpu.VMEM((piece_e, routed), F32),
-            pltpu.VMEM((n - 1, piece_d, routed), F32),
-            pltpu.VMEM((width, routed), F32),
-            pltpu.VMEM((width, routed), F32),
-            pltpu.VMEM(w_gateup.shape, BF16),
-            pltpu.VMEM((rows, width), BF16),
-            pltpu.VMEM((flight, cap, width), BF16),
-            pltpu.VMEM((flight, cap, routed), F32),
-            pltpu.VMEM((tok_count, routed), BF16),
-            dma((2, 3, n - 1)), dma((2, 3, n - 1)),
-            dma((flight - 1,)), dma((flight - 1,)),
-            dma((n - 1,)), dma((n - 1,)),
-            dma((n - 1,)), dma((n - 1,)),
-            dma((flight - 1,)), dma((flight - 1,)),
-            dma, dma((flight - 1,)), dma((flight - 1,)),
-            dma((flight - 1,)), dma((flight - 1,)),
-        ],
-        compiler_params=pltpu.CompilerParams(
-            collective_id=0, has_side_effects=True, vmem_limit_bytes=58 * 2**20
-        ),
-        cost_estimate=pl.CostEstimate(
-            flops=2 * rows * width * (gate_up + hidden),
-            bytes_accessed=2 * (width * gate_up + hidden * width) // n,
-            transcendentals=0,
-        ),
-        name="grads",
-    )(xt, pre_grad, ht, dyk, score, w_gateup, tokt, router_weight, logits, small, ids, spot, zw)
-
-def rows_kernel(
+def rows_part(
     flight, cap,
-    tok_ref, og_ref, rw_ref, ids_ref, wg_hbm, wd_hbm,
-    xt_ref, ht_ref, pg_ref, dy_ref, score_ref, logit_ref, small_ref, spot_ref,
+    tok_ref, og_ref, rw_ref, ids_ref, zw_ref, load_g, load_d, greet,
+    xt_ref, ht_ref, pg_ref, score_ref, logit_ref, small_ref, spot_ref,
     wg_ref, wd_ref, out_x, out_o, out_p, in_x, in_o, in_p, pre, hid,
-    wg_sem, wd_sem, x_send, x_recv, o_send, o_recv, p_send, p_recv,
+    x_send, x_recv, o_send, o_recv, p_send, p_recv,
 ):
     d = lax.axis_index("dp")
     e = lax.axis_index("expert")
-    load_g = pltpu.make_async_copy(wg_hbm, wg_ref, wg_sem)
-    load_d = pltpu.make_async_copy(wd_hbm, wd_ref, wd_sem)
-    load_g.start()
-    load_d.start()
-    barrier = pltpu.get_barrier_semaphore()
-    for k in range(1, flight):
-        pl.semaphore_signal(barrier, inc=1, device_id=(d, lax.rem(e + k, flight)), device_id_type=MESH)
-
-    tok_count, top = ids_ref.shape
+    top, tok_count = ids_ref.shape
     routed = rw_ref.shape[1]
     hidden_units, width = wd_ref.shape
     tile = min(hidden_units, 512)
     pairs = flight // 2
     lanes = lax.broadcasted_iota(jnp.int32, (tok_count, routed), 1)
-    choose = [ids_ref[:, k:k + 1] == lanes for k in range(top)]
+    def column(row):
+        return jnp.broadcast_to(row, (routed, tok_count)).T
+
+    ids = [column(ids_ref[k:k + 1, :].astype(F32)).astype(jnp.int32) for k in range(top)]
+    choose = [column_ids == lanes for column_ids in ids]
     member = sum(c.astype(F32) for c in choose)
     earlier = lax.broadcasted_iota(jnp.int32, (tok_count, tok_count), 0) > (
         lax.broadcasted_iota(jnp.int32, (tok_count, tok_count), 1)
@@ -386,7 +317,7 @@
     ranks = lax.broadcasted_iota(jnp.int32, (cap, tok_count), 0)
     picks = [by_expert[f:f + 1, :] == ranks for f in range(flight)]
 
-    pl.semaphore_wait(barrier, flight - 1)
+    greet()
 
     def rows_of(index):
         return pl.ds(pl.multiple_of(index * cap, cap), cap)
@@ -430,7 +361,7 @@
     norm = sum(chosen)
     probs = [c / norm for c in chosen]
     log_total = jnp.log(jnp.sum(jnp.exp(logits), axis=1, keepdims=True))
-    small = jnp.where(lanes == top, log_total, 0.0)
+    small = jnp.where(lanes == top, log_total, column(zw_ref[...]))
     spot = jnp.full(lanes.shape, -1, jnp.int32)
     weight = jnp.zeros(lanes.shape, F32)
     place = jnp.where((rank >= 0.0) & (lanes < flight), rank + (lanes * cap).astype(F32) + 1.0, 0.0)
@@ -438,6 +369,7 @@
         small = jnp.where(lanes == k, probs[k], small)
         at = jnp.sum(jnp.where(choose[k], place, 0.0), axis=1, keepdims=True) - 1.0
         spot = jnp.where(lanes == k, at.astype(jnp.int32), spot)
+        spot = jnp.where(lanes == top + k, ids[k], spot)
         weight = weight + jnp.where(choose[k], probs[k], 0.0)
     small_ref[...] = small
     spot_ref[...] = spot
@@ -464,24 +396,18 @@
         return pl.ds(pl.multiple_of(pair * (2 * cap), 2 * cap), 2 * cap)
 
     load_g.wait()
-
-    def forward(i, carry):
+    load_d.wait()
+
+    def one_pair(i, carry):
         pair = lax.rem(lax.div(e, 2) + i, pairs)
+        rows = pair_rows(pair)
         arrived([give_x], pair)
-        rows = pair_rows(pair)
         for col in range(0, 2 * hidden_units, tile):
-            pre[rows, col:col + tile] = jnp.dot(
+            pre[:, col:col + tile] = jnp.dot(
                 in_x[rows, :], wg_ref[:, col:col + tile], preferred_element_type=F32
             )
-        return carry
-
-    lax.fori_loop(0, pairs, forward, 0)
-    load_d.wait()
-
-    def backward(i, carry):
-        pair = lax.rem(lax.div(e, 2) + i, pairs)
+        xt_ref[:, rows] = in_x[rows, :].T
         arrived([give_o, give_p], pair)
-        rows = pair_rows(pair)
         prob = in_p[rows, 0:1]
         score = jnp.zeros((2 * cap, 1), F32)
         for col in range(0, hidden_units, tile):
@@ -489,12 +415,12 @@
                 in_o[rows, :], wd_ref[col:col + tile, :], (((1,), (1,)), ((), ())),
                 preferred_element_type=F32,
             )
-            gate = pre[rows, col:col + tile]
-            up = pre[rows, hidden_units + col:hidden_units + col + tile]
+            gate = pre[:, col:col + tile]
+            up = pre[:, hidden_units + col:hidden_units + col + tile]
             sig = jax.nn.sigmoid(gate)
             active = gate * sig
             hidden = (active * up).astype(BF16)
-            hid[rows, col:col + tile] = hidden
+            hid[:, col:col + tile] = hidden
             score = score + jnp.sum(raw * hidden.astype(F32), axis=1, keepdims=True)
             grad = prob * raw
             pg_ref[rows, col:col + tile] = (
@@ -502,43 +428,89 @@
             ).astype(BF16)
             pg_ref[rows, hidden_units + col:hidden_units + col + tile] = (grad * active).astype(BF16)
         score_ref[rows, :] = jnp.broadcast_to(score, (2 * cap, routed))
-        dy_ref[rows, :] = (prob * in_o[rows, :].astype(F32)).astype(BF16)
+        in_o[rows, :] = (prob * in_o[rows, :].astype(F32)).astype(BF16)
+        ht_ref[:, rows] = hid[...].T
         return carry
 
-    xt_ref[...] = in_x[...].T
-    lax.fori_loop(0, pairs, backward, 0)
-    ht_ref[...] = hid[...].T
+    lax.fori_loop(0, pairs, one_pair, 0)
     for to in peers():
         give_x(e, to).wait_send()
         give_o(e, to).wait_send()
         give_p(e, to).wait_send()
 
 
-def expert_rows(flight, tokens, out_grad, router_weight, ids, w_gateup, w_down):
+def layer_kernel(copies, flight, order, cap, *refs):
+    tok_ref, og_ref, rw_ref, ids_ref, zw_ref, wg_hbm, wd_hbm = refs[:7]
+    outs = refs[7:11]
+    xt, ht, pg, score, logit, small, spot, wg_ref, wd_ref = refs[11:20]
+    rows_scratch = refs[20:28]
+    wg_sem, wd_sem = refs[28:30]
+    rows_sems = refs[30:36]
+    grads_scratch = refs[36:]
+    out_x, in_x, dy = rows_scratch[0], rows_scratch[3], rows_scratch[4]
+    d = lax.axis_index("dp")
+    e = lax.axis_index("expert")
+    load_g = pltpu.make_async_copy(wg_hbm, wg_ref, wg_sem)
+    load_d = pltpu.make_async_copy(wd_hbm, wd_ref, wd_sem)
+    load_g.start()
+    load_d.start()
+    barrier = pltpu.get_barrier_semaphore()
+    for k in range(1, flight):
+        to = lax.rem(e + k, flight)
+        pl.semaphore_signal(barrier, inc=1, device_id=(d, to), device_id_type=MESH)
+    for k in range(1, copies):
+        to = lax.rem(d + k, copies)
+        pl.semaphore_signal(barrier, inc=1, device_id=(to, e), device_id_type=MESH)
+
+    def greet():
+        pl.semaphore_wait(barrier, copies + flight - 2)
+
+    rows_part(
+        flight, cap, tok_ref, og_ref, rw_ref, ids_ref, zw_ref, load_g, load_d, greet,
+        xt, ht, pg, score, logit, small, spot, wg_ref, wd_ref, *rows_scratch, *rows_sems,
+    )
+    grads_part(
+        copies, flight, order, ids_ref.shape[0],
+        tok_ref, rw_ref, wg_ref, xt, pg, ht, dy, score, logit, small, spot, out_x, in_x,
+        *outs, *grads_scratch,
+    )
+
+
+def per_device(tokens, out_grad, z_weight, router_weight, expert_ids, gate_up_weight, down_weight):
+    n = lax.axis_size("dp")
+    flight = lax.axis_size("expert")
+    w_gateup, w_down = gate_up_weight[0], down_weight[0]
     tok_count, width = tokens.shape
     routed = router_weight.shape[1]
     hidden = w_down.shape[0]
+    gate_up = w_gateup.shape[1]
     cap = tok_count // 2
     rows = flight * cap
+    gu_rows, dn_rows = width // n, hidden // n
+    piece_e = width // flight
+    piece_d = piece_e // n
     dma = pltpu.SemaphoreType.DMA
     vmem = pl.BlockSpec(memory_space=pltpu.VMEM)
     hbm = pl.BlockSpec(memory_space=pl.ANY)
     shape = jax.ShapeDtypeStruct
-    return pl.pallas_call(
-        functools.partial(rows_kernel, flight, cap),
+    gate_up_grad, down_grad, router_grad, token_grad = pl.pallas_call(
+        functools.partial(layer_kernel, n, flight, ring_order(n), cap),
         out_shape=(
-            shape((width, rows), BF16),
-            shape((hidden, rows), BF16),
-            shape((rows, 2 * hidden), BF16),
-            shape((rows, width), BF16),
-            shape((rows, routed), F32),
-            shape((tok_count, routed), F32),
-            shape((tok_count, routed), F32),
-            shape((tok_count, routed), jnp.int32),
+            shape((1, gu_rows, gate_up), BF16),
+            shape((1, dn_rows, width), BF16),
+            shape((width, routed), F32),
+            shape((tok_count, width), BF16),
         ),
-        in_specs=[vmem] * 4 + [hbm] * 2,
-        out_specs=(vmem,) * 8,
+        in_specs=[vmem] * 5 + [hbm] * 2,
+        out_specs=(vmem,) * 4,
         scratch_shapes=[
+            pltpu.VMEM((width, rows), BF16),
+            pltpu.VMEM((hidden, rows), BF16),
+            pltpu.VMEM((rows, gate_up), BF16),
+            pltpu.VMEM((rows, routed), F32),
+            pltpu.VMEM((tok_count, routed), F32),
+            pltpu.VMEM((tok_count, routed), F32),
+            pltpu.VMEM((tok_count, routed), jnp.int32),
             pltpu.VMEM(w_gateup.shape, BF16),
             pltpu.VMEM(w_down.shape, BF16),
             pltpu.VMEM((rows, width), BF16),
@@ -547,44 +519,39 @@
             pltpu.VMEM((rows, width), BF16),
             pltpu.VMEM((rows, width), BF16),
             pltpu.VMEM((rows, routed), F32),
-            pltpu.VMEM((rows, 2 * hidden), F32),
-            pltpu.VMEM((rows, hidden), BF16),
+            pltpu.VMEM((2 * cap, gate_up), F32),
+            pltpu.VMEM((2 * cap, hidden), BF16),
             dma, dma,
-        ] + [dma((flight,))] * 6,
+        ] + [dma((flight,))] * 6 + [
+            pltpu.VMEM((2, 2, n, gu_rows // 2, gate_up // 2), BF16),
+            pltpu.VMEM((2, n, dn_rows, width // 2), BF16),
+            pltpu.VMEM((flight - 1, piece_e, routed), F32),
+            pltpu.VMEM((piece_e, routed), BF16),
+            pltpu.VMEM((n - 1, piece_d, routed), BF16),
+            pltpu.VMEM((width, routed), F32),
+            pltpu.VMEM((width, routed), F32),
+            pltpu.VMEM((flight, cap, routed), F32),
+            pltpu.VMEM((tok_count, routed), BF16),
+            dma((2, 3, n - 1)), dma((2, 3, n - 1)),
+            dma((flight - 1,)), dma((flight - 1,)),
+            dma((n - 1,)), dma((n - 1,)),
+            dma((n - 1,)), dma((n - 1,)),
+            dma((flight - 1,)), dma((flight - 1,)),
+            dma((flight - 1,)), dma((flight - 1,)),
+            dma((flight - 1,)), dma((flight - 1,)),
+        ],
         compiler_params=pltpu.CompilerParams(
-            collective_id=1, has_side_effects=True, vmem_limit_bytes=58 * 2**20
+            collective_id=0, has_side_effects=True, vmem_limit_bytes=67_000_000
         ),
-        cost_estimate=pl.CostEstimate(
-            flops=6 * rows * width * hidden,
-            bytes_accessed=6 * width * hidden,
-            transcendentals=rows * hidden,
-        ),
-        name="rows",
-    )(tokens, out_grad, router_weight, ids, w_gateup, w_down)
-
-
-def per_device(tokens, out_grad, z_weight, router_weight, expert_ids, gate_up_weight, down_weight):
-    flight = lax.axis_size("expert")
-    w_gateup = gate_up_weight[0]
-    xt, ht, pre_grad, dyk, score, logits, small, spot = expert_rows(
-        flight, tokens, out_grad, router_weight, expert_ids, w_gateup, down_weight[0]
-    )
-    gate_up_grad, down_grad, router_grad, token_grad = reduce_grads(
-        lax.axis_size("dp"),
-        flight,
-        xt,
-        pre_grad,
-        ht,
-        dyk,
-        score,
+        name="layer",
+    )(
+        tokens,
+        out_grad,
+        router_weight,
+        expert_ids.T,
+        z_weight[None, :],
         w_gateup,
-        tokens.T,
-        router_weight,
-        logits,
-        small,
-        expert_ids,
-        spot,
-        z_weight[:, None],
+        w_down,
     )
     return (token_grad, router_grad, gate_up_grad, down_grad)
 

time: 245 us -> 234 us (0.955)
  Pallas kernels: 233 us -> 225 us
  local copies, waits for them, and re-layouts: 10.4 us -> 7.75 us
    pallas_call x2 -> x1, Pallas kernels: 233 us -> 225 us  [per_device(): pl.pallas_call(functools.partial(layer_kernel, n, flight, ring_order(n),...]
    unnamed x12 -> x6, local copies, waits for them, and re-layouts: 9.02 us -> 7.75 us
where the time goes in v4:
time: 234 us; the launch traced here: 233 us
  Pallas kernels  225 us (96%)
  local copies, waits for them, and re-layouts  7.75 us (3%)
    pallas_call x1, Pallas kernels, per_device(): pl.pallas_call(functools.partial(layer_kernel, n, flight, ring_order(n),...  225 us
    unnamed x6, local copies, waits for them, and re-layouts  7.75 us

profile of v4, /device:TPU:0, one launch (start us, length us, event | category | flops | bytes accessed | tf_op | source)
XLA Modules:
  0.0 233.3 jit_solution(8404535768373380952)
XLA Ops:
  0.6 224.9 %layer.1 = (bf16[1,256,3072]{2,1,0:T(8,128)(2,1)}, bf16[1,192,2048]{2,1,0:T(8,128)(2,1)}, f32[2048,128]{1,0:T(8,128)}, bf16[128,2048]{1,0:T(8,128)(2,1)}) custom-call(bf16[128,2048]{1,0:T(8,128)(2,1)} %refs_0_.1, bf16[128,2048]{1,0:T(8,128)(2,1)} %refs_1_.1, bf16[2048,128]{1,0:T(8,128)(2,1)} %refs_2_.1, s32[4,128]{1,0:T(4,128)} %bitcast.6, ...), custom_call_target="tpu_custom_call" | custom-call | tf_op jit(solution)/shard_map/layer/pallas_call | solution.py:496
  225.6 0.0 copy-start
  225.6 2.0 copy.15
  227.5 2.3 copy.16
  229.8 2.7 %copy.17 = bf16[1,256,3072]{2,1,0:T(8,128)(2,1)} copy(bf16[1,256,3072]{2,1,0:T(8,128)(2,1)} %get-tuple-element.18) | data formatting | bytes 3145728
  232.4 0.0 copy-done
  232.4 0.9 copy.18
Async XLA Ops:
  225.6 6.9 %copy-start = (bf16[1,192,2048]{2,1,0:T(8,128)(2,1)S(1)}, bf16[1,192,2048]{2,1,0:T(8,128)(2,1)}, u32[]{:S(2)}) copy-start(bf16[1,192,2048]{2,1,0:T(8,128)(2,1)} %get-tuple-element.19) | copy-start | bytes 2359300

commit v5 on v4

--- a/solution.py
+++ b/solution.py
@@ -474,6 +474,11 @@
         tok_ref, rw_ref, wg_ref, xt, pg, ht, dy, score, logit, small, spot, out_x, in_x,
         *outs, *grads_scratch,
     )
+
+
+def finish_kernel(*refs):
+    for source, target in zip(refs[:4], refs[4:]):
+        target[...] = source[...]
 
 
 def per_device(tokens, out_grad, z_weight, router_weight, expert_ids, gate_up_weight, down_weight):
@@ -553,7 +558,15 @@
         w_gateup,
         w_down,
     )
-    return (token_grad, router_grad, gate_up_grad, down_grad)
+    results = (token_grad, router_grad, gate_up_grad, down_grad)
+    return pl.pallas_call(
+        finish_kernel,
+        out_shape=tuple(shape(r.shape, r.dtype) for r in results),
+        in_specs=[vmem] * 4,
+        out_specs=(vmem,) * 4,
+        compiler_params=pltpu.CompilerParams(vmem_limit_bytes=16 * 2**20),
+        name="finish",
+    )(*results)
 
 
 def solution(mesh):

time: 234 us -> 233 us (level)
  local copies, waits for them, and re-layouts: 7.75 us -> 4.8 us
    unnamed x6 -> x8, local copies, waits for them, and re-layouts: 7.75 us -> 4.8 us
where the time goes in v5:
time: 233 us
  Pallas kernels  227 us (97%)
  local copies, waits for them, and re-layouts  4.8 us (2%)
    pallas_call x1, Pallas kernels, per_device(): pl.pallas_call(functools.partial(layer_kernel, n, flight, ring_order(n),...  225 us
    unnamed x8, local copies, waits for them, and re-layouts  4.8 us

profile of v5, /device:TPU:0, one launch (start us, length us, event | category | flops | bytes accessed | tf_op | source)
XLA Modules:
  0.0 232.5 jit_solution(11917615010227782740)
XLA Ops:
  0.6 224.9 %layer.1 = (bf16[1,256,3072]{2,1,0:T(8,128)(2,1)}, bf16[1,192,2048]{2,1,0:T(8,128)(2,1)}, f32[2048,128]{1,0:T(8,128)}, bf16[128,2048]{1,0:T(8,128)(2,1)}) custom-call(bf16[128,2048]{1,0:T(8,128)(2,1)} %refs_0_.1, bf16[128,2048]{1,0:T(8,128)(2,1)} %refs_1_.1, bf16[2048,128]{1,0:T(8,128)(2,1)} %refs_2_.1, s32[4,128]{1,0:T(4,128)} %bitcast.6, ...), custom_call_target="tpu_custom_call" | custom-call | tf_op jit(solution)/shard_map/layer/pallas_call | solution.py:501
  225.5 0.0 copy-start
  225.6 1.4 copy-done
  227.0 0.0 copy-start.1
  227.0 1.2 copy-done.1
  228.2 0.0 copy-start.2
  228.2 1.1 copy-done.2
  229.3 0.0 copy-start.3
  229.3 1.0 copy-done.3
  230.4 2.2 finish.1
Async XLA Ops:
  225.5 1.4 copy-start
  227.0 1.2 copy-start.1
  228.2 1.1 copy-start.2
  229.3 1.0 copy-start.3
